TPU v7x, 512 devices: a whole 4x8x8 slice. The times are simulated.
512 devices in a mesh: vox: 64 (over z, x, core), subj: 8 (over y).
Axes of the slice: x: 4, y: 8, z: 8, core: 2. Of those that a mesh axis runs over, the one named last changes fastest.
Arguments:
- series: bfloat16 [32, 16384, 512], P('subj', 'vox'), may hold values from -6 to 6
- live_mask: int32 [16384], P('vox'), may hold values from 0 to 1, as said below
- neighbours: int32 [16384, 13], P('vox'), may hold values from -1 to 510, as said below
- start_vectors: float32 [16384, 64], P('vox'), may hold values from -60 to 60
Outputs:
- embedding: float32 [16384, 64], P('vox')
Inputs may be any that keep to these rules, and one draw needn't show every extreme that they name: `live_mask`: within each aligned block of 128 voxel slots the live slots are a leading run of 1 to 128 slots. `neighbours`: slot n of voxel i names voxel (i // 256 - 1) * 256 + n, which is live and lies before i; the entries of a row are distinct or -1; rows of dead voxels are all -1; rows of the first 256 voxels name no slot under 256.
All inputs are finite; a program needn't handle non-finite values.
Results may differ from a plain program's by a relative error of at most 0.0024.
Values may be sent and summed in bfloat16 or wider, within the bound.
A program may use at most 64 MiB of HBM per device.

v0:
```python
import math

import jax
import jax.numpy as jnp
from jax import lax
from jax.sharding import PartitionSpec as P

ITERS = 3


def copy_for_each(shard, axis):
    copies = jnp.broadcast_to(shard, (lax.axis_size(axis), *shard.shape))
    return lax.all_to_all(copies, axis, split_axis=0, concat_axis=0, tiled=True)


def taken_together(shard, axis):
    return copy_for_each(shard, axis).sum(axis=0)


def shifted(shard, axis, by):
    count = lax.axis_size(axis)
    pairs = [(i, i + by) for i in range(count) if 0 <= i + by < count]
    return lax.ppermute(shard, axis, pairs)


def as_sent(shard):
    return jax.tree.map(lambda a: a.astype(jnp.bfloat16) if a.dtype == jnp.float32 else a, shard)


def standard(block):
    values = block.astype(jnp.float32)
    center = values - jnp.mean(values, axis=-1, keepdims=True)
    spread = jnp.mean(center * center, axis=-1, keepdims=True)
    return (center * lax.rsqrt(spread + 1e-05)).astype(jnp.bfloat16)


def orthonormal(images):
    gram_matrix = jnp.dot(images.T, images, precision=lax.Precision.HIGHEST)
    gram_matrix = taken_together(gram_matrix, "vox")
    factor = jnp.linalg.cholesky(gram_matrix)
    return lax.linalg.triangular_solve(
        factor, images, left_side=False, lower=True, transpose_a=True
    )


def dense_graph(weight, slots, columns_total):
    column_ids = jnp.arange(columns_total, dtype=jnp.int32)
    matrix = jnp.zeros((weight.shape[0], columns_total), jnp.float32)
    for offset in range(weight.shape[1]):
        hits = (slots[:, offset][:, None] == column_ids[None, :]).astype(jnp.float32)
        matrix = matrix + weight[:, offset][:, None] * hits
    return matrix


def product(left, right):
    return jnp.dot(left, right, precision=lax.Precision.HIGHEST)


def on_device(series, live_mask, neighbours, start_vectors):
    voxels_here = series.shape[1]
    frames = series.shape[2]
    subjects = series.shape[0] * lax.axis_size("subj")
    scale_factor = 0.5 / math.sqrt(frames * subjects)
    zscored = standard(series)
    earlier = shifted(zscored, "vox", 1)
    window = jnp.concatenate([earlier, zscored], axis=1)
    present = neighbours >= 0
    safe_slots = jnp.maximum(neighbours, 0)
    columns = []
    for offset in range(neighbours.shape[1]):
        picked = jnp.take(window, safe_slots[:, offset], axis=1)
        columns.append(
            jnp.einsum("svf,svf->v", zscored, picked, preferred_element_type=jnp.float32)
        )
    partial_sums = jnp.stack(columns, axis=1)
    summed = taken_together(partial_sums, "subj")
    weight = jnp.where(present, jnp.exp(scale_factor * summed), 0.0)
    living = live_mask.astype(jnp.float32)
    local_graph = dense_graph(weight, neighbours, 2 * voxels_here)
    owed = jnp.sum(local_graph, axis=0)
    received = shifted(owed[:voxels_here], "vox", -1)
    degree = 1.0 + jnp.sum(weight, axis=1) + owed[voxels_here:] + received
    scaling = living * lax.rsqrt(degree)
    vectors = living[:, None] * start_vectors
    for repeat in range(ITERS):
        scaled = scaling[:, None] * vectors
        earlier_rows = shifted(as_sent(scaled), "vox", 1).astype(scaled.dtype)
        window_rows = jnp.concatenate([earlier_rows, scaled], axis=0)
        forward = product(local_graph, window_rows)
        returns = product(local_graph.T, scaled)
        arrived = shifted(as_sent(returns[:voxels_here]), "vox", -1)
        images = 0.5 * (
            vectors + scaling[:, None] * (scaled + forward + returns[voxels_here:] + arrived)
        )
        vectors = orthonormal(images)
    return vectors


def solution(mesh):
    placed = (P("subj", "vox", None), P("vox"), P("vox", None), P("vox", None))
    return jax.shard_map(
        on_device, mesh=mesh, in_specs=placed, out_specs=P("vox", None), check_vma=False
    )
```

profile of v0, /device:TPU:1, one launch (start us, length us, event | category | flops | bytes accessed | tf_op | source)
XLA Modules:
  0.0 317.2 jit_solution(3449821898318450883)
XLA Ops:
  0.0 2.1 convert_reduce_fusion
  2.2 1.2 fusion.2
  3.4 1.6 fusion.3
  5.0 4.7 %collective-permute-start = (bf16[4,256,512]{2,0,1:T(4,128)(2,1)S(1)}, bf16[4,256,512]{2,0,1:T(4,128)(2,1)S(1)}, u32[]{:S(2)}, u32[]{:S(2)}) collective-permute-start(bf16[4,256,512]{2,0,1:T(4,128)(2,1)S(1)} %fusion.3), channel_id=1, source_target_pairs={{0,8},{8,16},{16,24},{24,32},{32,40},{40,48},{48,56},{56,64},{64,7... | collective-permute-start | bytes 3145736 | tf_op jit(solution)/shard_map/ppermute | solution.py:23
  10.2 11.0 %collective-permute-done = bf16[4,256,512]{2,0,1:T(4,128)(2,1)S(1)} collective-permute-done((bf16[4,256,512]{2,0,1:T(4,128)(2,1)S(1)}, bf16[4,256,512]{2,0,1:T(4,128)(2,1)S(1)}, u32[]{:S(2)}, u32[]{:S(2)}) %collective-permute-start) | collective-permute-done | bytes 1048608 | tf_op jit(solution)/shard_map/ppermute | solution.py:23
  21.2 1.4 pad_maximum_fusion
  22.6 2.5 gather_fusion.3
  25.0 2.5 gather_fusion.2
  27.5 2.5 gather_fusion.1
  30.0 2.5 gather_fusion
  32.5 2.5 gather_fusion.12
  34.9 2.5 gather_fusion.11
  37.4 2.5 gather_fusion.10
  39.9 2.5 gather_fusion.9
  42.3 2.5 gather_fusion.8
  44.9 2.5 gather_fusion.7
  47.3 2.7 gather_fusion.6
  50.0 2.4 gather_fusion.5
  52.5 2.5 gather_fusion.4
  55.0 9.5 %fusion.7 = (f32[256]{0:T(256)S(1)}, f32[256]{0:T(256)S(1)}, f32[256]{0:T(256)S(1)}, f32[256]{0:T(256)S(1)}) fusion(bf16[256,4,512]{2,1,0:T(4,128)(2,1)} %gather_fusion.3, pred[256]{0:T(512)(128)(4,1)S(1)} %get-tuple-element.72, bf16[256,4,512]{2,1,0:T(4,128)(2,1)} %gather_fusion.2, pred[256]{0:T(512)(128)(4,1)S(1)} %get-tuple-element.73, ...), kind=kLoop, calls=%fused_computation.35 | loop fusion | flops 11009024 | bytes 5256192 | tf_op jit(solution)/shard_map/svf,svf->v/dot_general | solution.py:73
  64.6 14.7 %fusion.16 = (f32[256]{0:T(256)S(1)}, f32[256]{0:T(256)S(1)}, f32[256]{0:T(256)S(1)}, f32[256]{0:T(256)S(1)}, f32[256]{0:T(256)S(1)}, /*index=5*/f32[256]{0:T(25...) fusion(bf16[256,4,512]{2,1,0:T(4,128)(2,1)S(1)} %copy-done.1, pred[256]{0:T(512)(128)(4,1)S(1)} %get-tuple-element.76, ...), kind=kLoop, calls=%fused_computation.44 | loop fusion | flops 21493504 | bytes 10505472 | tf_op jit(solution)/shard_map/svf,svf->v/dot_general | solution.py:73
  79.3 0.6 broadcast_in_dim.21
  80.0 6.8 %all-to-all-start = ((f32[8,256,13]{1,2,0:T(8,128)}), f32[8,256,13]{1,2,0:T(8,128)S(1)}, u32[]{:S(2)}, u32[]{:S(2)}) async-start(f32[8,256,13]{1,2,0:T(8,128)} %broadcast_in_dim.21), calls=%async_computation | async-start | bytes 262144 | tf_op jit(solution)/shard_map/all_to_all | solution.py:13
  86.8 7.9 %all-to-all-done = f32[8,256,13]{1,2,0:T(8,128)S(1)} async-done(((f32[8,256,13]{1,2,0:T(8,128)}), f32[8,256,13]{1,2,0:T(8,128)S(1)}, u32[]{:S(2)}, u32[]{:S(2)}) %all-to-all-start) | async-done | bytes 106528 | tf_op jit(solution)/shard_map/all_to_all | solution.py:13
  94.8 1.0 fusion.61
  95.8 1.9 collective-permute-start.1
  97.7 5.1 %collective-permute-done.1 = f32[256]{0:T(256)S(1)} collective-permute-done((f32[256]{0:T(256)S(1)}, f32[256]{0:T(256)S(1)}, u32[]{:S(2)}, u32[]{:S(2)}) %collective-permute-start.1) | collective-permute-done | bytes 1056 | tf_op jit(solution)/shard_map/ppermute | solution.py:23
  102.8 2.0 collective-permute-start.2
  105.3 2.4 collective-permute-start.3
  107.7 2.8 collective-permute-done.3
  110.5 0.6 fusion.31
  111.6 2.3 reshape.222
  113.9 47.4 %all_to_all.20 = f32[64,1,4096]{2,1,0:T(1,128)S(1)} all-to-all(f32[64,1,4096]{2,1,0:T(1,128)} %reshape.222), channel_id=1, replica_groups=mesh['vox'=64,'subj'=8] {'vox'}, dimensions={0} | all-to-all | bytes 2097152 | tf_op jit(solution)/shard_map/all_to_all | solution.py:13
  161.8 4.5 %reduce.30 = f32[64,4096]{1,0:T(8,128)} reduce(f32[64,1,4096]{2,1,0:T(1,128)S(1)} %all_to_all.20, f32[]{:T(128)} %broadcast.240), dimensions={1}, to_apply=%all_to_all.13.reduce_sub_computation | reduce | bytes 2097156 | tf_op jit(solution)/shard_map/all_to_all | solution.py:13
  166.3 2.0 reshape.223
  168.6 5.8 %cholesky.59 = f32[64,64]{1,0:T(8,128)S(1)} custom-call(f32[64,64]{1,0:T(8,128)S(1)} %fusion.49), custom_call_target="Cholesky" | custom-call | tf_op jit(solution)/shard_map/jit(cholesky)/cholesky | solution.py:40
  174.4 0.7 compare_reduce_fusion.2
  175.2 0.7 fusion.41
  175.9 4.9 %custom-call.7 = f32[1,64,64]{1,2,0:T(8,128)S(1)} custom-call(f32[1,64,64]{2,1,0:T(8,128)S(1)} %fusion.41), custom_call_target="InvertDiagBlocksLowerTriangular" | custom-call | tf_op jit(solution)/shard_map/triangular_solve/custom-call.0 | solution.py:41
  181.1 4.1 %collective-permute-start.4 = (bf16[256,64]{0,1:T(8,128)(2,1)S(1)}, bf16[256,64]{0,1:T(8,128)(2,1)S(1)}, u32[]{:S(2)}, u32[]{:S(2)}) collective-permute-start(bf16[256,64]{0,1:T(8,128)(2,1)S(1)} %get-tuple-element.23), channel_id=1, source_target_pairs={{0,8},{8,16},{16,24},{24,32},{32,40},{40,48},{48,56},{56,64},{64,7... | collective-permute-start | bytes 98312 | tf_op jit(solution)/shard_map/ppermute | solution.py:23
  185.7 1.9 collective-permute-start.5
  187.6 3.3 %collective-permute-done.5 = bf16[256,64]{0,1:T(8,128)(2,1)S(1)} collective-permute-done((bf16[256,64]{0,1:T(8,128)(2,1)S(1)}, bf16[256,64]{0,1:T(8,128)(2,1)S(1)}, u32[]{:S(2)}, u32[]{:S(2)}) %collective-permute-start.5) | collective-permute-done | bytes 32800 | tf_op jit(solution)/shard_map/ppermute | solution.py:23
  190.9 0.6 fusion.26
  192.0 2.3 reshape.224
  194.3 37.0 %all_to_all.21 = f32[64,1,4096]{2,1,0:T(1,128)S(1)} all-to-all(f32[64,1,4096]{2,1,0:T(1,128)} %reshape.224), channel_id=1, replica_groups=mesh['vox'=64,'subj'=8] {'vox'}, dimensions={0} | all-to-all | bytes 2097152 | tf_op jit(solution)/shard_map/all_to_all | solution.py:13
  231.3 4.5 %reduce.31 = f32[64,4096]{1,0:T(8,128)} reduce(f32[64,1,4096]{2,1,0:T(1,128)S(1)} %all_to_all.21, f32[]{:T(128)} %broadcast.240), dimensions={1}, to_apply=%all_to_all.14.reduce_sub_computation | reduce | bytes 2097156 | tf_op jit(solution)/shard_map/all_to_all | solution.py:13
  235.8 2.0 reshape.225
  238.0 5.8 %cholesky.70 = f32[64,64]{1,0:T(8,128)S(1)} custom-call(f32[64,64]{1,0:T(8,128)S(1)} %fusion.47), custom_call_target="Cholesky" | custom-call | tf_op jit(solution)/shard_map/jit(cholesky)/cholesky | solution.py:40
  243.9 0.7 compare_reduce_fusion.1
  244.6 0.7 fusion.42
  245.3 4.9 %custom-call.8 = f32[1,64,64]{1,2,0:T(8,128)S(1)} custom-call(f32[1,64,64]{2,1,0:T(8,128)S(1)} %fusion.42), custom_call_target="InvertDiagBlocksLowerTriangular" | custom-call | tf_op jit(solution)/shard_map/triangular_solve/custom-call.0 | solution.py:41
  250.5 4.1 %collective-permute-start.6 = (bf16[256,64]{0,1:T(8,128)(2,1)S(1)}, bf16[256,64]{0,1:T(8,128)(2,1)S(1)}, u32[]{:S(2)}, u32[]{:S(2)}) collective-permute-start(bf16[256,64]{0,1:T(8,128)(2,1)S(1)} %get-tuple-element.21), channel_id=1, source_target_pairs={{0,8},{8,16},{16,24},{24,32},{32,40},{40,48},{48,56},{56,64},{64,7... | collective-permute-start | bytes 98312 | tf_op jit(solution)/shard_map/ppermute | solution.py:23
  255.1 1.9 collective-permute-start.7
  257.1 3.3 %collective-permute-done.7 = bf16[256,64]{0,1:T(8,128)(2,1)S(1)} collective-permute-done((bf16[256,64]{0,1:T(8,128)(2,1)S(1)}, bf16[256,64]{0,1:T(8,128)(2,1)S(1)}, u32[]{:S(2)}, u32[]{:S(2)}) %collective-permute-start.7) | collective-permute-done | bytes 32800 | tf_op jit(solution)/shard_map/ppermute | solution.py:23
  260.4 0.6 fusion.21
  261.5 1.3 reshape.226
  262.8 36.9 %all_to_all.22 = f32[64,1,4096]{2,1,0:T(1,128)S(1)} all-to-all(f32[64,1,4096]{2,1,0:T(1,128)S(1)} %reshape.226), channel_id=1, replica_groups=mesh['vox'=64,'subj'=8] {'vox'}, dimensions={0} | all-to-all | bytes 2097152 | tf_op jit(solution)/shard_map/all_to_all | solution.py:13
  299.6 3.3 %reduce.32 = f32[64,4096]{1,0:T(8,128)S(1)} reduce(f32[64,1,4096]{2,1,0:T(1,128)S(1)} %all_to_all.22, f32[]{:T(128)} %broadcast.240), dimensions={1}, to_apply=%all_to_all.15.reduce_sub_computation | reduce | bytes 2097156 | tf_op jit(solution)/shard_map/all_to_all | solution.py:13
  302.9 0.8 reshape.227
  304.0 5.8 %cholesky.81 = f32[64,64]{1,0:T(8,128)S(1)} custom-call(f32[64,64]{1,0:T(8,128)S(1)} %fusion.45), custom_call_target="Cholesky" | custom-call | tf_op jit(solution)/shard_map/jit(cholesky)/cholesky | solution.py:40
  309.9 0.6 compare_reduce_fusion
  310.5 0.7 fusion.43
  311.2 4.9 %custom-call.9 = f32[1,64,64]{1,2,0:T(8,128)S(1)} custom-call(f32[1,64,64]{2,1,0:T(8,128)S(1)} %fusion.43), custom_call_target="InvertDiagBlocksLowerTriangular" | custom-call | tf_op jit(solution)/shard_map/triangular_solve/custom-call.0 | solution.py:41
  316.1 0.9 convolution_bitcast_fusion
  (97 shorter events, 5.1 us)
Async XLA Ops:
  0.0 2.2 copy-start
  2.1 7.6 %copy-start.7 = (s32[256,13]{0,1:T(8,128)S(1)}, s32[256,13]{0,1:T(8,128)}, u32[]{:S(2)}) copy-start(s32[256,13]{0,1:T(8,128)} %param.11) | copy-start | bytes 39940
  5.0 16.2 %collective-permute-start = (bf16[4,256,512]{2,0,1:T(4,128)(2,1)S(1)}, bf16[4,256,512]{2,0,1:T(4,128)(2,1)S(1)}, u32[]{:S(2)}, u32[]{:S(2)}) collective-permute-start(bf16[4,256,512]{2,0,1:T(4,128)(2,1)S(1)} %fusion.3), channel_id=1, source_target_pairs={{0,8},{8,16},{16,24},{24,32},{32,40},{40,48},{48,56},{56,64},{64,7... | collective-permute-start | bytes 3145736 | tf_op jit(solution)/shard_map/ppermute | solution.py:23
  55.0 9.5 %copy-start.1 = (bf16[256,4,512]{2,1,0:T(4,128)(2,1)S(1)}, bf16[256,4,512]{2,1,0:T(4,128)(2,1)}, u32[]{:S(2)}) copy-start(bf16[256,4,512]{2,1,0:T(4,128)(2,1)} %gather_fusion.12) | copy-start | bytes 3145732
  55.0 9.5 %copy-start.2 = (bf16[256,4,512]{2,1,0:T(4,128)(2,1)S(1)}, bf16[256,4,512]{2,1,0:T(4,128)(2,1)}, u32[]{:S(2)}) copy-start(bf16[256,4,512]{2,1,0:T(4,128)(2,1)} %gather_fusion.11) | copy-start | bytes 3145732
  55.0 9.5 %copy-start.3 = (bf16[256,4,512]{2,1,0:T(4,128)(2,1)S(1)}, bf16[256,4,512]{2,1,0:T(4,128)(2,1)}, u32[]{:S(2)}) copy-start(bf16[256,4,512]{2,1,0:T(4,128)(2,1)} %gather_fusion.10) | copy-start | bytes 3145732
  55.0 9.5 %copy-start.4 = (bf16[256,4,512]{2,1,0:T(4,128)(2,1)S(1)}, bf16[256,4,512]{2,1,0:T(4,128)(2,1)}, u32[]{:S(2)}) copy-start(bf16[256,4,512]{2,1,0:T(4,128)(2,1)} %gather_fusion.9) | copy-start | bytes 3145732
  55.0 9.5 %copy-start.5 = (bf16[256,4,512]{2,1,0:T(4,128)(2,1)S(1)}, bf16[256,4,512]{2,1,0:T(4,128)(2,1)}, u32[]{:S(2)}) copy-start(bf16[256,4,512]{2,1,0:T(4,128)(2,1)} %gather_fusion.8) | copy-start | bytes 3145732
  64.6 33.1 %copy-start.8 = (s32[256]{0:T(256)S(1)}, s32[256]{0:T(256)}, u32[]{:S(2)}) copy-start(s32[256]{0:T(256)} %param.10) | copy-start | bytes 3076
  64.6 38.2 %copy-start.6 = (f32[256,64]{0,1:T(8,128)S(1)}, f32[256,64]{0,1:T(8,128)}, u32[]{:S(2)}) copy-start(f32[256,64]{0,1:T(8,128)} %param.12) | copy-start | bytes 196612
  80.0 14.8 %all-to-all-start = ((f32[8,256,13]{1,2,0:T(8,128)}), f32[8,256,13]{1,2,0:T(8,128)S(1)}, u32[]{:S(2)}, u32[]{:S(2)}) async-start(f32[8,256,13]{1,2,0:T(8,128)} %broadcast_in_dim.21), calls=%async_computation | async-start | bytes 262144 | tf_op jit(solution)/shard_map/all_to_all | solution.py:13
  95.8 7.0 %collective-permute-start.1 = (f32[256]{0:T(256)S(1)}, f32[256]{0:T(256)S(1)}, u32[]{:S(2)}, u32[]{:S(2)}) collective-permute-start(f32[256]{0:T(256)S(1)} %slice.190), channel_id=1, source_target_pairs={{8,0},{16,8},{24,16},{32,24},{40,32},{48,40},{56,48},{64,56},{72,6... | collective-permute-start | bytes 3080 | tf_op jit(solution)/shard_map/ppermute | solution.py:23
  102.8 4.8 %collective-permute-start.2 = (bf16[256,64]{0,1:T(8,128)(2,1)S(1)}, bf16[256,64]{0,1:T(8,128)(2,1)S(1)}, u32[]{:S(2)}, u32[]{:S(2)}) collective-permute-start(bf16[256,64]{0,1:T(8,128)(2,1)S(1)} %get-tuple-element.25), channel_id=1, source_target_pairs={{0,8},{8,16},{16,24},{24,32},{32,40},{40,48},{48,56},{56,64},{64,7... | collective-permute-start | bytes 98312 | tf_op jit(solution)/shard_map/ppermute | solution.py:23
  105.3 5.2 %collective-permute-start.3 = (bf16[256,64]{0,1:T(8,128)(2,1)S(1)}, bf16[256,64]{0,1:T(8,128)(2,1)S(1)}, u32[]{:S(2)}, u32[]{:S(2)}) collective-permute-start(bf16[256,64]{0,1:T(8,128)(2,1)S(1)} %slice.264), channel_id=1, source_target_pairs={{8,0},{16,8},{24,16},{32,24},{40,32},{48,40},{56,48},{64,56},{72,6... | collective-permute-start | bytes 98312 | tf_op jit(solution)/shard_map/ppermute | solution.py:23
  181.1 6.6 %collective-permute-start.4 = (bf16[256,64]{0,1:T(8,128)(2,1)S(1)}, bf16[256,64]{0,1:T(8,128)(2,1)S(1)}, u32[]{:S(2)}, u32[]{:S(2)}) collective-permute-start(bf16[256,64]{0,1:T(8,128)(2,1)S(1)} %get-tuple-element.23), channel_id=1, source_target_pairs={{0,8},{8,16},{16,24},{24,32},{32,40},{40,48},{48,56},{56,64},{64,7... | collective-permute-start | bytes 98312 | tf_op jit(solution)/shard_map/ppermute | solution.py:23
  185.7 5.2 %collective-permute-start.5 = (bf16[256,64]{0,1:T(8,128)(2,1)S(1)}, bf16[256,64]{0,1:T(8,128)(2,1)S(1)}, u32[]{:S(2)}, u32[]{:S(2)}) collective-permute-start(bf16[256,64]{0,1:T(8,128)(2,1)S(1)} %slice.263), channel_id=1, source_target_pairs={{8,0},{16,8},{24,16},{32,24},{40,32},{48,40},{56,48},{64,56},{72,6... | collective-permute-start | bytes 98312 | tf_op jit(solution)/shard_map/ppermute | solution.py:23
  250.5 6.6 %collective-permute-start.6 = (bf16[256,64]{0,1:T(8,128)(2,1)S(1)}, bf16[256,64]{0,1:T(8,128)(2,1)S(1)}, u32[]{:S(2)}, u32[]{:S(2)}) collective-permute-start(bf16[256,64]{0,1:T(8,128)(2,1)S(1)} %get-tuple-element.21), channel_id=1, source_target_pairs={{0,8},{8,16},{16,24},{24,32},{32,40},{40,48},{48,56},{56,64},{64,7... | collective-permute-start | bytes 98312 | tf_op jit(solution)/shard_map/ppermute | solution.py:23
  255.1 5.2 %collective-permute-start.7 = (bf16[256,64]{0,1:T(8,128)(2,1)S(1)}, bf16[256,64]{0,1:T(8,128)(2,1)S(1)}, u32[]{:S(2)}, u32[]{:S(2)}) collective-permute-start(bf16[256,64]{0,1:T(8,128)(2,1)S(1)} %slice.262), channel_id=1, source_target_pairs={{8,0},{16,8},{24,16},{32,24},{40,32},{48,40},{56,48},{64,56},{72,6... | collective-permute-start | bytes 98312 | tf_op jit(solution)/shard_map/ppermute | solution.py:23
where the time goes:
time: 321 us; the launch traced here: 317 us
  blocking collectives  121 us (38%)
  other arithmetic  80.9 us (25%)
  local copies, waits for them, and re-layouts  45.4 us (14%)
  waiting for transfers between devices  33.4 us (10%)
  starting transfers between devices  29.9 us (9%)
  matrix products  5.25 us (2%)
    all_to_all x3, blocking collectives, copy_for_each(): return lax.all_to_all(copies, axis, split_axis=0, concat_axis=0, tiled=True)  121 us
    gather x13, local copies, waits for them, and re-layouts, on_device(): picked = jnp.take(window, safe_slots[:, offset], axis=1)  32.5 us
    ppermute x8, waiting for transfers between devices, shifted(): return lax.ppermute(shard, axis, pairs)  25.5 us
    dot_general x2, other arithmetic, on_device(): jnp.einsum('svf,svf->v', zscored, picked, preferred_element_type=jnp.floa...  24.2 us
    ppermute x8, starting transfers between devices, shifted(): return lax.ppermute(shard, axis, pairs)  23.1 us
    another operation x9, other arithmetic, orthonormal(): factor = jnp.linalg.cholesky(gram_matrix)  19.7 us
    another operation x6, other arithmetic, orthonormal(): lax.linalg.triangular_solve(factor, images, left_side=False, lower=True,...  16.7 us
    all_to_all x3, other arithmetic, copy_for_each(): return lax.all_to_all(copies, axis, split_axis=0, concat_axis=0, tiled=True)  12.2 us
  transfers between devices with their start and end apart: 9, of which 6 were waited for; matrix products, arithmetic and copies ran while one was open for 1% of the time, Pallas kernels for 0%

commit v1 on v0

v1 whole, which is shorter than its diff:
```python
import functools
import math

import jax
import jax.numpy as jnp
from jax import lax
from jax.experimental import pallas as pl
from jax.experimental.pallas import tpu as pltpu
from jax.sharding import PartitionSpec as P

ITERS = 3
HIGHEST = lax.Precision.HIGHEST
NN = (((1,), (0,)), ((), ()))
NT = (((1,), (1,)), ((), ()))


def matmul(left, right, dims, precision=None):
    return lax.dot_general(
        left, right, dims, precision=precision, preferred_element_type=jnp.float32
    )


def split(values):
    high = values.astype(jnp.bfloat16)
    low = (values - high.astype(jnp.float32)).astype(jnp.bfloat16)
    return high, low


def factor_inverse(rows):
    total, width = rows.shape
    sublane = lax.broadcasted_iota(jnp.int32, (8, width), 0)
    done = []
    for first in range(0, total, 8):
        left = total - first
        cols = [
            jnp.broadcast_to(rows[:, first + c : first + c + 1], (left, width))
            for c in range(8)
        ]
        block = jnp.zeros((8, width), jnp.float32)
        for c in range(8):
            root = lax.rsqrt(cols[c][c : c + 1, :])
            lower = cols[c] * root
            pivot = rows[c : c + 1, :] * root
            block = jnp.where(sublane == c, pivot, block)
            rows = rows - lower * pivot
            for other in range(c + 1, 8):
                cols[other] = cols[other] - lower * lower[other : other + 1, :]
        done.append(block)
        rows = rows[8:]
    return jnp.concatenate(done, axis=0)


def kernel(
    sizes,
    series_ref,
    mask_ref,
    near_ref,
    start_ref,
    out_ref,
    raw,
    zown,
    zprev,
    near,
    live,
    begin,
    corr,
    part,
    parts,
    ghigh,
    glow,
    owed,
    owing,
    scale_row,
    image,
    ahead,
    ahead_in,
    back,
    back_in,
    gram,
    stage1,
    half,
    stage2,
    whole,
    other,
    in_sems,
    z_send,
    z_recv,
    part_send,
    part_recv,
    owed_sems,
    halo_send,
    halo_recv,
    s1_send,
    s1_recv,
    s2_send,
    s2_recv,
    s3_sems,
):
    groups, plane, planes, scale_factor = sizes
    count = plane * planes
    subjects, voxels, frames = series_ref.shape
    offsets = near_ref.shape[0]
    vecs = start_ref.shape[0]
    me = lax.axis_index("vox")
    group = lax.axis_index("subj")
    spot = lax.rem(me, plane)
    level = me // plane
    core = lax.rem(me, 2)
    following = lax.rem(me + 1, count)
    previous = lax.rem(me + count - 1, count)
    partner = me + 1 - 2 * core

    plane_peers = [lax.rem(spot + d, plane) for d in range(1, plane)]
    level_peers = [lax.rem(level + d, planes) for d in range(1, planes)]
    group_peers = [lax.rem(group + d, groups) for d in range(1, groups)]

    loads = [
        pltpu.make_async_copy(series_ref.at[s], raw.at[s], in_sems.at[s])
        for s in range(subjects)
    ]
    small = [
        pltpu.make_async_copy(near_ref, near, in_sems.at[subjects]),
        pltpu.make_async_copy(mask_ref, live, in_sems.at[subjects + 1]),
        pltpu.make_async_copy(start_ref, begin, in_sems.at[subjects + 2]),
    ]
    for load in loads + small:
        load.start()

    barrier = pltpu.get_barrier_semaphore()
    targets = [{"vox": following}, {"vox": previous}]
    targets += [{"vox": level * plane + p} for p in plane_peers]
    targets += [{"vox": p * plane + spot} for p in level_peers]
    targets += [{"subj": p} for p in group_peers]
    for target in targets:
        pl.semaphore_signal(
            barrier, inc=1, device_id=target, device_id_type=pl.DeviceIdType.MESH
        )

    def remote(src, dst, send, recv, target):
        return pltpu.make_async_remote_copy(
            src_ref=src,
            dst_ref=dst,
            send_sem=send,
            recv_sem=recv,
            device_id=target,
            device_id_type=pl.DeviceIdType.MESH,
        )

    step = 32
    z_copies = []
    for s in range(subjects):
        loads[s].wait()

        @pl.loop(0, voxels // step)
        def _(r):
            rows = pl.ds(pl.multiple_of(r * step, step), step)
            values = raw[s, rows, :].astype(jnp.float32)
            center = values - jnp.mean(values, axis=-1, keepdims=True)
            spread = jnp.mean(center * center, axis=-1, keepdims=True)
            zown[s, rows, :] = (center * lax.rsqrt(spread + 1e-05)).astype(jnp.bfloat16)

        if s == 0:
            pl.semaphore_wait(barrier, len(targets))
        copy = remote(
            zown.at[s], zprev.at[s], z_send.at[s], z_recv.at[s], {"vox": following}
        )
        copy.start()
        z_copies.append(copy)
        local = matmul(zown[s], zown[s], NT)
        if s == 0:
            corr[voxels:, :] = local
        else:
            corr[voxels:, :] += local
    for load in small:
        load.wait()

    tile = lax.broadcasted_iota(jnp.int32, (8, voxels), 0)
    slots = [jnp.broadcast_to(near[k : k + 1, :], (8, voxels)) for k in range(offsets)]

    def picked(first, last, sums):
        def body(r, sums):
            ids = tile + r * 8
            values = corr[pl.ds(pl.multiple_of(r * 8, 8), 8), :]
            return tuple(
                total + jnp.where(ids == slots[k], values, 0.0)
                for k, total in enumerate(sums)
            )

        return lax.fori_loop(first // 8, last // 8, body, sums, unroll=2)

    sums = tuple(jnp.zeros((8, voxels), jnp.float32) for _ in range(offsets))
    sums = picked(voxels, 2 * voxels, sums)
    for s in range(subjects):
        z_copies[s].wait_recv()
        cross = matmul(zprev[s], zown[s], NT)
        if s == 0:
            corr[:voxels, :] = cross
        else:
            corr[:voxels, :] += cross
    sums = picked(0, voxels, sums)
    part[...] = jnp.zeros(part.shape, jnp.float32)
    for k in range(offsets):
        part[k : k + 1, :] = jnp.sum(sums[k], axis=0, keepdims=True)

    part_copies = []
    for d, peer in enumerate(group_peers):
        copy = remote(
            part, parts.at[group], part_send.at[d], part_recv.at[group], {"subj": peer}
        )
        copy.start()
        part_copies.append(copy)
    parts[group] = part[...]
    vectors = live[...].astype(jnp.float32) * begin[...]
    for d, peer in enumerate(group_peers):
        remote(
            part, parts.at[peer], part_send.at[d], part_recv.at[peer], {"subj": peer}
        ).wait_recv()
    summed = parts[0]
    for g in range(1, groups):
        summed = summed + parts[g]
    weight = [
        jnp.where(
            near[k : k + 1, :] >= 0, jnp.exp(scale_factor * summed[k : k + 1, :]), 0.0
        )
        for k in range(offsets)
    ]
    listed = weight[0]
    for k in range(1, offsets):
        listed = listed + weight[k]
    spread_weight = [jnp.broadcast_to(w, (8, voxels)) for w in weight]

    @pl.loop(0, 2 * voxels // 16)
    def _(r):
        tiles = []
        for h in range(2):
            ids = tile + (r * 16 + h * 8)
            entry = jnp.zeros((8, voxels), jnp.float32)
            for k in range(offsets):
                entry = jnp.where(ids == slots[k], spread_weight[k], entry)
            tiles.append(entry)
        high, low = split(jnp.concatenate(tiles, axis=0))
        rows = pl.ds(pl.multiple_of(r * 16, 16), 16)
        ghigh[rows, :] = high
        glow[rows, :] = low

    ones = jnp.ones((8, voxels), jnp.bfloat16)
    columns = matmul(ones, ghigh[...], NT) + matmul(ones, glow[...], NT)
    owed[...] = columns[:, :voxels]
    owed_copy = remote(owed, owing, owed_sems.at[0], owed_sems.at[1], {"vox": previous})
    owed_copy.start()
    owed_copy.wait_recv()
    degree = 1.0 + listed + columns[:1, voxels:] + owing[:1, :]
    scale_row[...] = live[...].astype(jnp.float32) * lax.rsqrt(degree)

    def halo(t):
        return (
            remote(
                ahead.at[t], ahead_in.at[t], halo_send.at[t, 0], halo_recv.at[t, 0],
                {"vox": following},
            ),
            remote(
                back.at[t], back_in.at[t], halo_send.at[t, 1], halo_recv.at[t, 1],
                {"vox": previous},
            ),
        )

    def send_halo(t, current):
        scaled = scale_row[...] * current
        ahead[t] = scaled
        forward, backward = halo(t)
        forward.start()
        high, low = split(scaled)
        both = jnp.concatenate([high, low], axis=0)
        first = matmul(both, ghigh[:voxels, :], NT)
        back[t] = first[:vecs] + first[vecs:] + matmul(high, glow[:voxels, :], NT)
        backward.start()

    def apply(t, current):
        scaled = scale_row[...] * current
        high, low = split(scaled)
        both = jnp.concatenate([high, low], axis=0)
        mine = matmul(both, ghigh[voxels:, :], NT) + matmul(both, ghigh[voxels:, :], NN)
        rest = matmul(high, glow[voxels:, :], NT) + matmul(high, glow[voxels:, :], NN)
        for copy in halo(t):
            copy.wait_recv()
        early_high, early_low = split(ahead_in[t])
        early = jnp.concatenate([early_high, early_low], axis=0)
        mine = mine + matmul(early, ghigh[:voxels, :], NN)
        rest = rest + matmul(early_high, glow[:voxels, :], NN)
        total = scaled + mine[:vecs] + mine[vecs:] + rest + back_in[t]
        return 0.5 * (current + scale_row[...] * total)

    send_halo(0, vectors)
    image[...] = apply(0, vectors)

    lane = lax.broadcasted_iota(jnp.int32, (vecs // 2, 2 * vecs), 1)
    row = lax.broadcasted_iota(jnp.int32, (vecs // 2, 2 * vecs), 0)
    quarter = vecs // 4

    def stage1_copy(t, d, arriving=False):
        peer = plane_peers[d]
        source = gram.at[t, pl.ds(pl.multiple_of(lax.rem(peer, 2) * quarter, quarter), quarter)]
        target = {"vox": level * plane + peer}
        slot = peer if arriving else spot
        return remote(source, stage1.at[t, slot], s1_send.at[t, d], s1_recv.at[t, slot], target)

    def stage2_copy(t, d, arriving=False):
        peer = level_peers[d]
        target = {"vox": peer * plane + spot}
        slot = peer if arriving else level
        return remote(half.at[t], stage2.at[t, slot], s2_send.at[t, d], s2_recv.at[t, slot], target)

    def stage3_copy(t):
        return remote(whole.at[t], other.at[t], s3_sems.at[t, 0], s3_sems.at[t, 1], {"vox": partner})

    def iterate(t):
        current = image[...]
        twice = jnp.concatenate([current, current], axis=0)
        product = matmul(current, twice, NT, HIGHEST)
        packed = jnp.where(lane < vecs, product[: vecs // 2], product[vecs // 2 :])
        gram[t] = packed
        for d in range(plane - 1):
            stage1_copy(t, d).start()
        own = pl.ds(pl.multiple_of(core * quarter, quarter), quarter)
        stage1[t, spot] = gram[t, own]

        @pl.when(t < ITERS - 1)
        def _():
            send_halo(t + 1, current)

        for d in range(plane - 1):
            stage1_copy(t, d, True).wait_recv()
        total = stage1[t, 0]
        for p in range(1, plane):
            total = total + stage1[t, p]
        half[t] = total
        for d in range(planes - 1):
            stage2_copy(t, d).start()
        stage2[t, level] = total

        @pl.when(t < ITERS - 1)
        def _():
            image[...] = apply(t + 1, current)

        for d in range(planes - 1):
            stage2_copy(t, d, True).wait_recv()
        total = stage2[t, 0]
        for p in range(1, planes):
            total = total + stage2[t, p]
        whole[t] = total
        exchange = stage3_copy(t)
        exchange.start()
        exchange.wait_recv()
        got = other[t]
        upper = jnp.where(core == 0, total, got)
        lower = jnp.where(core == 0, got, total)
        full = jnp.concatenate([upper, lower], axis=0)
        top = jnp.where(lane < vecs, full, (lane - vecs == row).astype(jnp.float32))
        bottom = jnp.where(
            lane < vecs,
            pltpu.roll(full, vecs, 1),
            (lane - vecs == row + vecs // 2).astype(jnp.float32),
        )
        solved = factor_inverse(jnp.concatenate([top, bottom], axis=0))
        inverse = pltpu.roll(solved, vecs, 1)[:, :vecs]
        image[...] = matmul(inverse, image[...], NN, HIGHEST)

    pl.loop(0, ITERS)(iterate)
    out_ref[...] = image[...]

    for copy in z_copies + part_copies + [owed_copy]:
        copy.wait_send()
    for t in range(ITERS):
        for copy in halo(t):
            copy.wait_send()
        for d in range(plane - 1):
            stage1_copy(t, d).wait_send()
        for d in range(planes - 1):
            stage2_copy(t, d).wait_send()
        stage3_copy(t).wait_send()


def solution(mesh):
    count, groups = mesh.shape["vox"], mesh.shape["subj"]
    plane = 8 if count >= 16 else count // 2
    planes = count // plane

    def on_device(series, live_mask, neighbours, start_vectors):
        subjects, voxels, frames = series.shape
        vecs = start_vectors.shape[1]
        offsets = neighbours.shape[1]
        scale_factor = 0.5 / math.sqrt(frames * subjects * groups)
        f32, bf16, i32 = jnp.float32, jnp.bfloat16, jnp.int32
        block = (vecs, voxels)
        quarter = (vecs // 4, 2 * vecs)
        dma = pltpu.SemaphoreType.DMA
        anywhere = pl.BlockSpec(memory_space=pl.ANY)
        result = pl.pallas_call(
            functools.partial(kernel, (groups, plane, planes, scale_factor)),
            out_shape=jax.ShapeDtypeStruct(block, f32),
            in_specs=[anywhere] * 4,
            out_specs=pl.BlockSpec(memory_space=pltpu.VMEM),
            scratch_shapes=[
                pltpu.VMEM((subjects, voxels, frames), bf16),
                pltpu.VMEM((subjects, voxels, frames), bf16),
                pltpu.VMEM((subjects, voxels, frames), bf16),
                pltpu.VMEM((offsets, voxels), i32),
                pltpu.VMEM((1, voxels), i32),
                pltpu.VMEM(block, f32),
                pltpu.VMEM((2 * voxels, voxels), f32),
                pltpu.VMEM((16, voxels), f32),
                pltpu.VMEM((groups, 16, voxels), f32),
                pltpu.VMEM((2 * voxels, voxels), bf16),
                pltpu.VMEM((2 * voxels, voxels), bf16),
                pltpu.VMEM((8, voxels), f32),
                pltpu.VMEM((8, voxels), f32),
                pltpu.VMEM((1, voxels), f32),
                pltpu.VMEM(block, f32),
                pltpu.VMEM((ITERS, *block), f32),
                pltpu.VMEM((ITERS, *block), f32),
                pltpu.VMEM((ITERS, *block), f32),
                pltpu.VMEM((ITERS, *block), f32),
                pltpu.VMEM((ITERS, vecs // 2, 2 * vecs), f32),
                pltpu.VMEM((ITERS, plane, *quarter), f32),
                pltpu.VMEM((ITERS, *quarter), f32),
                pltpu.VMEM((ITERS, planes, *quarter), f32),
                pltpu.VMEM((ITERS, *quarter), f32),
                pltpu.VMEM((ITERS, *quarter), f32),
                dma((subjects + 3,)),
                dma((subjects,)),
                dma((subjects,)),
                dma((max(groups - 1, 1),)),
                dma((groups,)),
                dma((2,)),
                dma((ITERS, 2)),
                dma((ITERS, 2)),
                dma((ITERS, plane - 1)),
                dma((ITERS, plane)),
                dma((ITERS, planes - 1)),
                dma((ITERS, planes)),
                dma((ITERS, 2)),
            ],
            compiler_params=pltpu.CompilerParams(
                collective_id=0, has_side_effects=True, vmem_limit_bytes=32 << 20
            ),
        )(series, live_mask.reshape(1, voxels), neighbours.T, start_vectors.T)
        return result.T

    placed = (P("subj", "vox", None), P("vox"), P("vox", None), P("vox", None))
    return jax.shard_map(
        on_device, mesh=mesh, in_specs=placed, out_specs=P("vox", None), check_vma=False
    )
```

time: 321 us -> 87.3 us (0.27); the launches traced: 317 us -> 87 us
  blocking collectives: 121 us -> 0 us
  Pallas kernels: 0 us -> 82.9 us
  other arithmetic: 80.9 us -> 0 us
  local copies, waits for them, and re-layouts: 45.4 us -> 4.09 us
  waiting for transfers between devices: 33.4 us -> 0 us
  starting transfers between devices: 29.9 us -> 0 us
  matrix products: 5.25 us -> 0 us
    all_to_all x3 -> x0, blocking collectives: 121 us -> none  [copy_for_each(): return lax.all_to_all(copies, axis, split_axis=0, concat_axis=0, tiled=True)]
    pallas_call x0 -> x1, Pallas kernels: none -> 82.9 us  [on_device(): pl.pallas_call(functools.partial(kernel, (groups, plane, planes, scale_fa...]
    another operation x15 -> x0, other arithmetic: 36.5 us -> none  [the longest x9 19.7 us: orthonormal(): factor = jnp.linalg.cholesky(gram_matrix)]
    gather x13 -> x0, local copies, waits for them, and re-layouts: 32.5 us -> none  [on_device(): picked = jnp.take(window, safe_slots[:, offset], axis=1)]
    ppermute x8 -> x0, waiting for transfers between devices: 25.5 us -> none  [shifted(): return lax.ppermute(shard, axis, pairs)]
    dot_general x2 -> x0, other arithmetic: 24.2 us -> none  [on_device(): jnp.einsum('svf,svf->v', zscored, picked, preferred_element_type=jnp.floa...]
    ppermute x8 -> x0, starting transfers between devices: 23.1 us -> none  [shifted(): return lax.ppermute(shard, axis, pairs)]
    all_to_all x3 -> x0, other arithmetic: 12.2 us -> none  [copy_for_each(): return lax.all_to_all(copies, axis, split_axis=0, concat_axis=0, tiled=True)]
  transfers between devices with their start and end apart: 9 -> 0, of which waited for: 6 -> 0; matrix products, arithmetic and copies ran while one was open for 1% -> 0% of each run, Pallas kernels for 0% -> 0%
where the time goes in v1:
time: 87.3 us; the launch traced here: 87 us
  Pallas kernels  82.9 us (95%)
  local copies, waits for them, and re-layouts  4.09 us (5%)
    pallas_call x1, Pallas kernels, on_device(): pl.pallas_call(functools.partial(kernel, (groups, plane, planes, scale_fa...  82.9 us
    unnamed x9, local copies, waits for them, and re-layouts  4.09 us

profile of v1, /device:TPU:1, one launch (start us, length us, event | category | flops | bytes accessed | tf_op | source)
XLA Modules:
  0.0 87.0 jit_solution(3511130701411220412)
XLA Ops:
  0.0 0.0 copy-start.3
  0.0 0.7 copy-done.3
  0.7 0.0 copy-start
  0.7 1.2 %copy-done = bf16[4,256,512]{2,1,0:T(8,128)(2,1)S(1)} copy-done((bf16[4,256,512]{2,1,0:T(8,128)(2,1)S(1)}, bf16[4,256,512]{2,1,0:T(8,128)(2,1)}, u32[]{:S(2)}) %copy-start) | copy-done | bytes 1048600
  1.9 0.0 copy-start.1
  1.9 0.8 copy-done.1
  2.7 0.0 copy-start.2
  2.7 0.7 copy-done.2
  3.5 82.9 %shard_map.46 = f32[64,256]{1,0:T(8,128)S(1)} custom-call(bf16[4,256,512]{2,1,0:T(8,128)(2,1)S(1)} %copy-done, s32[1,256]{1,0:T(1,128)S(1)} %bitcast.7, s32[13,256]{1,0:T(8,128)S(1)} %bitcast.6, f32[64,256]{1,0:T(8,128)S(1)} %bitcast.5), custom_call_target="tpu_custom_call" | custom-call | tf_op jit(solution)/shard_map/pallas_call | solution.py:398
  86.4 0.6 copy.6
Async XLA Ops:
  0.0 0.7 copy-start.3
  0.7 1.2 %copy-start = (bf16[4,256,512]{2,1,0:T(8,128)(2,1)S(1)}, bf16[4,256,512]{2,1,0:T(8,128)(2,1)}, u32[]{:S(2)}) copy-start(bf16[4,256,512]{2,1,0:T(8,128)(2,1)} %series_ref.1) | copy-start | bytes 3145732
  1.9 0.8 copy-start.1
  2.7 0.7 copy-start.2

commit v2 on v1

v2 whole, which is shorter than its diff:
```python
import functools
import math

import jax
import jax.numpy as jnp
from jax import lax
from jax.experimental import pallas as pl
from jax.experimental.pallas import tpu as pltpu
from jax.sharding import PartitionSpec as P

ITERS = 3
HIGHEST = lax.Precision.HIGHEST
NN = (((1,), (0,)), ((), ()))
NT = (((1,), (1,)), ((), ()))


def matmul(left, right, dims, precision=None):
    return lax.dot_general(
        left, right, dims, precision=precision, preferred_element_type=jnp.float32
    )


def split(values):
    high = values.astype(jnp.bfloat16)
    low = (values - high.astype(jnp.float32)).astype(jnp.bfloat16)
    return high, low


def factor_inverse(rows):
    total, width = rows.shape
    sublane = lax.broadcasted_iota(jnp.int32, (8, width), 0)
    done = []
    for first in range(0, total, 8):
        left = total - first
        cols = [
            jnp.broadcast_to(rows[:, first + c : first + c + 1], (left, width))
            for c in range(8)
        ]
        block = jnp.zeros((8, width), jnp.float32)
        for c in range(8):
            root = lax.rsqrt(cols[c][c : c + 1, :])
            lower = cols[c] * root
            pivot = rows[c : c + 1, :] * root
            block = jnp.where(sublane == c, pivot, block)
            rows = rows - lower * pivot
            for other in range(c + 1, 8):
                cols[other] = cols[other] - lower * lower[other : other + 1, :]
        done.append(block)
        rows = rows[8:]
    return jnp.concatenate(done, axis=0)


def kernel(
    sizes,
    series_ref,
    mask_ref,
    near_ref,
    start_ref,
    out_ref,
    raw,
    zown,
    zahead,
    zback,
    near,
    near_next,
    live,
    begin,
    corr,
    corr_next,
    part_next,
    part_in,
    part,
    parts,
    listed,
    listed_next,
    ghigh,
    glow,
    nhigh,
    nlow,
    scale_row,
    scale_prev,
    scale_next,
    halo_out,
    from_prev,
    from_next,
    gram,
    stage1,
    half,
    stage2,
    whole,
    other,
    in_sems,
    send,
    recv,
    part_send,
    part_recv,
    halo_send,
    halo_recv,
    s1_send,
    s1_recv,
    s2_send,
    s2_recv,
    s3_sems,
):
    groups, plane, planes, scale_factor = sizes
    count = plane * planes
    subjects, voxels, frames = series_ref.shape
    offsets = near_ref.shape[0]
    vecs = start_ref.shape[0]
    halves, width = 2 * subjects, frames // 2
    passed = zahead.shape[0]
    me = lax.axis_index("vox")
    group = lax.axis_index("subj")
    spot = lax.rem(me, plane)
    level = me // plane
    core = lax.rem(me, 2)
    following = {"vox": lax.rem(me + 1, count)}
    previous = {"vox": lax.rem(me + count - 1, count)}
    partner = {"vox": me + 1 - 2 * core}

    plane_peers = [lax.rem(spot + d, plane) for d in range(1, plane)]
    level_peers = [lax.rem(level + d, planes) for d in range(1, planes)]
    group_peers = [lax.rem(group + d, groups) for d in range(1, groups)]

    order = [0] + list(range(subjects - 1, 0, -1))
    loads = [
        pltpu.make_async_copy(series_ref.at[s], raw.at[s], in_sems.at[s])
        for s in range(subjects)
    ]
    small = [
        pltpu.make_async_copy(near_ref, near, in_sems.at[subjects]),
        pltpu.make_async_copy(mask_ref, live, in_sems.at[subjects + 1]),
        pltpu.make_async_copy(start_ref, begin, in_sems.at[subjects + 2]),
    ]
    loads[0].start()
    for load in small:
        load.start()
    for s in order[1:]:
        loads[s].start()

    barrier = pltpu.get_barrier_semaphore()
    targets = [following, previous]
    targets += [{"vox": level * plane + p} for p in plane_peers]
    targets += [{"vox": p * plane + spot} for p in level_peers]
    targets += [{"subj": p} for p in group_peers]
    for target in targets:
        pl.semaphore_signal(
            barrier, inc=1, device_id=target, device_id_type=pl.DeviceIdType.MESH
        )

    def remote(src, dst, send_sem, recv_sem, target):
        return pltpu.make_async_remote_copy(
            src_ref=src,
            dst_ref=dst,
            send_sem=send_sem,
            recv_sem=recv_sem,
            device_id=target,
            device_id_type=pl.DeviceIdType.MESH,
        )

    def single(index, src, dst, target):
        return remote(src, dst, send.at[index], recv.at[index], target)

    def standardize(s):
        step = 64
        for r in range(0, voxels, step):
            values = raw[s, r : r + step, :].astype(jnp.float32)
            center = values - jnp.mean(values, axis=-1, keepdims=True)
            spread = jnp.mean(center * center, axis=-1, keepdims=True)
            result = (center * lax.rsqrt(spread + 1e-05)).astype(jnp.bfloat16)
            zown[2 * s, r : r + step, :] = result[:, :width]
            zown[2 * s + 1, r : r + step, :] = result[:, width:]

    with jax.named_scope("zscore"):
        loads[0].wait()
        standardize(0)
        with jax.named_scope("barrier"):
            pl.semaphore_wait(barrier, len(targets))
        first_on = single(0, zown.at[0:2], zahead.at[0:2], following)
        first_on.start()
        for load in small:
            load.wait()
        near_copy = single(3, near, near_next, previous)
        near_copy.start()
        turn = passed // 2
        for s in order[1 : subjects - turn + 1]:
            loads[s].wait()
            standardize(s)
        back_copy = single(2, zown.at[passed:halves], zback, previous)
        back_copy.start()
        for s in order[subjects - turn + 1 :]:
            loads[s].wait()
            standardize(s)
        rest_on = single(1, zown.at[2:passed], zahead.at[2:passed], following)
        rest_on.start()

    def products(left, right, first, last, left_first=0, right_first=0):
        total = None
        for h in range(first, last):
            term = matmul(left[left_first + h], right[right_first + h], NT)
            total = term if total is None else total + term
        return total

    tile = lax.broadcasted_iota(jnp.int32, (8, voxels), 0)

    def slots_of(ref):
        return [jnp.broadcast_to(ref[k : k + 1, :], (8, voxels)) for k in range(offsets)]

    def picked(source, slots, first, last, sums):
        def body(r, sums):
            ids = tile + r * 8
            values = source[pl.ds(pl.multiple_of(r * 8, 8), 8), :]
            return tuple(
                total + jnp.where(ids == slots[k], values, 0.0)
                for k, total in enumerate(sums)
            )

        return lax.fori_loop(first // 8, last // 8, body, sums, unroll=2)

    def down(sums, target):
        for k in range(offsets):
            target[k : k + 1, :] = jnp.sum(sums[k], axis=0, keepdims=True)

    nothing = tuple(jnp.zeros((8, voxels), jnp.float32) for _ in range(offsets))
    with jax.named_scope("pick_own"):
        corr[voxels:, :] = products(zown, zown, 0, halves)
        sums = picked(corr, slots_of(near), voxels, 2 * voxels, nothing)
        down(sums, part)
        vectors = live[...].astype(jnp.float32) * begin[...]
        halo_out[0] = vectors
    with jax.named_scope("wait_first"):
        first_on.wait_recv()
    corr[:voxels, :] = products(zahead, zown, 0, 2)
    with jax.named_scope("wait_back"):
        near_copy.wait_recv()
        back_copy.wait_recv()
    with jax.named_scope("pick_next"):
        corr_next[...] = products(zown, zback, 0, halves - passed, left_first=passed)
        down(picked(corr_next, slots_of(near_next), 0, voxels, nothing), part_next)
    next_copy = single(4, part_next, part_in, following)
    next_copy.start()
    with jax.named_scope("wait_rest"):
        rest_on.wait_recv()
    with jax.named_scope("pick_cross"):
        corr[:voxels, :] += products(zahead, zown, 2, passed)
        down(picked(corr, slots_of(near), 0, voxels, sums), part)
    with jax.named_scope("wait_part"):
        next_copy.wait_recv()
    part[...] += part_in[...]

    part_copies = []
    for d, peer in enumerate(group_peers):
        copy = remote(
            part, parts.at[group], part_send.at[d], part_recv.at[group], {"subj": peer}
        )
        copy.start()
        part_copies.append(copy)

    def halo(t):
        return (
            remote(halo_out.at[t], from_prev.at[t], halo_send.at[t, 0], halo_recv.at[t, 0], following),
            remote(halo_out.at[t], from_next.at[t], halo_send.at[t, 1], halo_recv.at[t, 1], previous),
        )

    for copy in halo(0):
        copy.start()
    parts[group] = part[...]
    with jax.named_scope("subj_wait"):
        for d, peer in enumerate(group_peers):
            remote(
                part, parts.at[peer], part_send.at[d], part_recv.at[peer], {"subj": peer}
            ).wait_recv()
    summed = parts[0]
    for g in range(1, groups):
        summed = summed + parts[g]
    weight = jnp.where(near[...] >= 0, jnp.exp(scale_factor * summed), 0.0)
    listed[...] = weight
    list_copy = single(5, listed, listed_next, previous)
    list_copy.start()

    def dense(near_table, weight_table, high_out, low_out, rows_total):
        slots, weights = slots_of(near_table), slots_of(weight_table)

        @pl.loop(0, rows_total // 16)
        def _(r):
            tiles = []
            for h in range(2):
                ids = tile + (r * 16 + h * 8)
                entry = jnp.zeros((8, voxels), jnp.float32)
                for k in range(offsets):
                    entry = jnp.where(ids == slots[k], weights[k], entry)
                tiles.append(entry)
            high, low = split(jnp.concatenate(tiles, axis=0))
            rows = pl.ds(pl.multiple_of(r * 16, 16), 16)
            high_out[rows, :] = high
            low_out[rows, :] = low

    ones = jnp.ones((8, voxels), jnp.bfloat16)
    with jax.named_scope("dense"):
        dense(near, listed, ghigh, glow, 2 * voxels)
        owed = matmul(ones, ghigh[voxels:, :], NT) + matmul(ones, glow[voxels:, :], NT)
    with jax.named_scope("wait_list"):
        list_copy.wait_recv()
    with jax.named_scope("degree"):
        dense(near_next, listed_next, nhigh, nlow, voxels)
        owed = owed + (matmul(ones, nhigh[...], NT) + matmul(ones, nlow[...], NT))
        degree = 1.0 + jnp.sum(listed[...], axis=0, keepdims=True) + owed[:1, :]
        scale_row[...] = live[...].astype(jnp.float32) * lax.rsqrt(degree)
    scale_copies = [
        single(6, scale_row, scale_prev, following),
        single(7, scale_row, scale_next, previous),
    ]
    for copy in scale_copies:
        copy.start()

    def stacked(values):
        high, low = split(values)
        return high, jnp.concatenate([high, low], axis=0)

    def own_part(current):
        scaled = scale_row[...] * current
        high, both = stacked(scaled)
        mine = matmul(both, ghigh[voxels:, :], NT) + matmul(both, ghigh[voxels:, :], NN)
        rest = matmul(high, glow[voxels:, :], NT) + matmul(high, glow[voxels:, :], NN)
        return scaled + (mine[:vecs] + mine[vecs:] + rest)

    def whole_part(current, own, before, after):
        high, both = stacked(before)
        mine = matmul(both, ghigh[:voxels, :], NN)
        rest = matmul(high, glow[:voxels, :], NN)
        high, both = stacked(after)
        mine = mine + matmul(both, nhigh[...], NT)
        rest = rest + matmul(high, nlow[...], NT)
        total = own + (mine[:vecs] + mine[vecs:] + rest)
        return 0.5 * (current + scale_row[...] * total)

    own = own_part(vectors)
    with jax.named_scope("wait_scale"):
        for copy in scale_copies + list(halo(0)):
            copy.wait_recv()
    images = whole_part(
        vectors, own, scale_prev[...] * from_prev[0], scale_next[...] * from_next[0]
    )

    lane = lax.broadcasted_iota(jnp.int32, (vecs // 2, 2 * vecs), 1)
    row_all = lax.broadcasted_iota(jnp.int32, (vecs, 2 * vecs), 0)
    lane_all = lax.broadcasted_iota(jnp.int32, (vecs, 2 * vecs), 1)
    identity = (lane_all - vecs == row_all).astype(jnp.float32)
    quarter = vecs // 4

    def send_halo(t, current):
        halo_out[t] = scale_row[...] * current
        for copy in halo(t):
            copy.start()

    def next_images(t, current):
        own = own_part(current)
        with jax.named_scope("wait_halo"):
            for copy in halo(t):
                copy.wait_recv()
        return whole_part(current, own, from_prev[t], from_next[t])

    def stage1_copy(t, d, arriving=False):
        peer = plane_peers[d]
        source = gram.at[t, pl.ds(pl.multiple_of(lax.rem(peer, 2) * quarter, quarter), quarter)]
        target = {"vox": level * plane + peer}
        slot = peer if arriving else spot
        return remote(source, stage1.at[t, slot], s1_send.at[t, d], s1_recv.at[t, slot], target)

    def stage2_copy(t, d, arriving=False):
        peer = level_peers[d]
        target = {"vox": peer * plane + spot}
        slot = peer if arriving else level
        return remote(half.at[t], stage2.at[t, slot], s2_send.at[t, d], s2_recv.at[t, slot], target)

    def stage3_copy(t):
        return remote(whole.at[t], other.at[t], s3_sems.at[t, 0], s3_sems.at[t, 1], partner)

    def sum_start(t, current):
        twice = jnp.concatenate([current, current], axis=0)
        product = matmul(current, twice, NT, HIGHEST)
        gram[t] = jnp.where(lane < vecs, product[: vecs // 2], product[vecs // 2 :])
        for d in range(plane - 1):
            stage1_copy(t, d).start()
        own_rows = pl.ds(pl.multiple_of(core * quarter, quarter), quarter)
        stage1[t, spot] = gram[t, own_rows]

    def sum_planes(t):
        with jax.named_scope(f"s1_wait{t}"):
            for d in range(plane - 1):
                stage1_copy(t, d, True).wait_recv()
        total = stage1[t, 0]
        for p in range(1, plane):
            total = total + stage1[t, p]
        half[t] = total
        for d in range(planes - 1):
            stage2_copy(t, d).start()
        stage2[t, level] = total

    def sum_levels(t):
        with jax.named_scope(f"s2_wait{t}"):
            for d in range(planes - 1):
                stage2_copy(t, d, True).wait_recv()
        total = stage2[t, 0]
        for p in range(1, planes):
            total = total + stage2[t, p]
        whole[t] = total
        stage3_copy(t).start()

    def sum_end(t):
        with jax.named_scope(f"s3_wait{t}"):
            stage3_copy(t).wait_recv()
        total, got = whole[t], other[t]
        upper = jnp.where(core == 0, total, got)
        lower = jnp.where(core == 0, got, total)
        full = jnp.concatenate([upper, lower], axis=0)
        return jnp.concatenate([full, pltpu.roll(full, vecs, 1)], axis=0)

    def inverse_factor(matrix):
        solved = factor_inverse(jnp.where(lane_all < vecs, matrix, identity))
        return pltpu.roll(solved, vecs, 1)[:, :vecs]

    def normalized(inverse, matrix):
        left = matmul(inverse, matrix[:, :vecs], NN, HIGHEST)
        padded = jnp.concatenate([inverse, jnp.zeros_like(inverse)], axis=0)
        return matmul(left, padded, NT, HIGHEST)

    sum_start(0, images)
    send_halo(1, images)
    sum_planes(0)
    images = next_images(1, images)
    sum_start(1, images)
    sum_levels(0)
    sum_planes(1)
    matrix = sum_end(0)
    with jax.named_scope("chol0"):
        inverse = inverse_factor(matrix)
    images = matmul(inverse, images, NN, HIGHEST)
    send_halo(2, images)
    images = next_images(2, images)
    sum_start(2, images)
    sum_levels(1)
    sum_planes(2)
    matrix = sum_end(1)
    with jax.named_scope("chol1"):
        inverse = inverse_factor(normalized(inverse, matrix))
    images = matmul(inverse, images, NN, HIGHEST)
    sum_levels(2)
    matrix = sum_end(2)
    with jax.named_scope("chol2"):
        inverse = inverse_factor(normalized(inverse, matrix))
    out_ref[...] = matmul(inverse, images, NN, HIGHEST)

    with jax.named_scope("tail"):
        singles = [first_on, rest_on, back_copy, near_copy, next_copy, list_copy]
        for copy in singles + scale_copies + part_copies:
            copy.wait_send()
        for t in range(ITERS):
            for copy in halo(t):
                copy.wait_send()
            for d in range(plane - 1):
                stage1_copy(t, d).wait_send()
            for d in range(planes - 1):
                stage2_copy(t, d).wait_send()
            stage3_copy(t).wait_send()


def solution(mesh):
    count, groups = mesh.shape["vox"], mesh.shape["subj"]
    plane = 8 if count >= 16 else count // 2
    planes = count // plane

    def on_device(series, live_mask, neighbours, start_vectors):
        subjects, voxels, frames = series.shape
        vecs = start_vectors.shape[1]
        offsets = neighbours.shape[1]
        scale_factor = 0.5 / math.sqrt(frames * subjects * groups)
        f32, bf16, i32 = jnp.float32, jnp.bfloat16, jnp.int32
        block = (vecs, voxels)
        table = (offsets, voxels)
        line = (1, voxels)
        quarter = (vecs // 4, 2 * vecs)
        halves, width = 2 * subjects, frames // 2
        passed = halves * 5 // 8
        dma = pltpu.SemaphoreType.DMA
        anywhere = pl.BlockSpec(memory_space=pl.ANY)
        result = pl.pallas_call(
            functools.partial(kernel, (groups, plane, planes, scale_factor)),
            out_shape=jax.ShapeDtypeStruct(block, f32),
            in_specs=[anywhere] * 4,
            out_specs=pl.BlockSpec(memory_space=pltpu.VMEM),
            scratch_shapes=[
                pltpu.VMEM((subjects, voxels, frames), bf16),
                pltpu.VMEM((halves, voxels, width), bf16),
                pltpu.VMEM((passed, voxels, width), bf16),
                pltpu.VMEM((halves - passed, voxels, width), bf16),
                pltpu.VMEM(table, i32),
                pltpu.VMEM(table, i32),
                pltpu.VMEM(line, i32),
                pltpu.VMEM(block, f32),
                pltpu.VMEM((2 * voxels, voxels), f32),
                pltpu.VMEM((voxels, voxels), f32),
                pltpu.VMEM(table, f32),
                pltpu.VMEM(table, f32),
                pltpu.VMEM(table, f32),
                pltpu.VMEM((groups, *table), f32),
                pltpu.VMEM(table, f32),
                pltpu.VMEM(table, f32),
                pltpu.VMEM((2 * voxels, voxels), bf16),
                pltpu.VMEM((2 * voxels, voxels), bf16),
                pltpu.VMEM((voxels, voxels), bf16),
                pltpu.VMEM((voxels, voxels), bf16),
                pltpu.VMEM(line, f32),
                pltpu.VMEM(line, f32),
                pltpu.VMEM(line, f32),
                pltpu.VMEM((ITERS, *block), f32),
                pltpu.VMEM((ITERS, *block), f32),
                pltpu.VMEM((ITERS, *block), f32),
                pltpu.VMEM((ITERS, vecs // 2, 2 * vecs), f32),
                pltpu.VMEM((ITERS, plane, *quarter), f32),
                pltpu.VMEM((ITERS, *quarter), f32),
                pltpu.VMEM((ITERS, planes, *quarter), f32),
                pltpu.VMEM((ITERS, *quarter), f32),
                pltpu.VMEM((ITERS, *quarter), f32),
                dma((subjects + 3,)),
                dma((8,)),
                dma((8,)),
                dma((max(groups - 1, 1),)),
                dma((groups,)),
                dma((ITERS, 2)),
                dma((ITERS, 2)),
                dma((ITERS, plane - 1)),
                dma((ITERS, plane)),
                dma((ITERS, planes - 1)),
                dma((ITERS, planes)),
                dma((ITERS, 2)),
            ],
            compiler_params=pltpu.CompilerParams(
                collective_id=0, has_side_effects=True
            ),
        )(series, live_mask.reshape(1, voxels), neighbours.T, start_vectors.T)
        return result.T

    placed = (P("subj", "vox", None), P("vox"), P("vox", None), P("vox", None))
    return jax.shard_map(
        on_device, mesh=mesh, in_specs=placed, out_specs=P("vox", None), check_vma=False
    )
```

time: 87.3 us -> 73.9 us (0.85)
  Pallas kernels: 82.9 us -> 72.2 us
  local copies, waits for them, and re-layouts: 4.09 us -> 1.47 us
    pallas_call x1, Pallas kernels: 82.9 us -> 72.2 us  [on_device(): pl.pallas_call(functools.partial(kernel, (groups, plane, planes, scale_fa...]
    unnamed x9 -> x1, local copies, waits for them, and re-layouts: 4.09 us -> 1.47 us
where the time goes in v2:
time: 73.9 us; the launch traced here: 73.7 us
  Pallas kernels  72.2 us (98%)
  local copies, waits for them, and re-layouts  1.47 us (2%)
    pallas_call x1, Pallas kernels, on_device(): pl.pallas_call(functools.partial(kernel, (groups, plane, planes, scale_fa...  72.2 us

profile of v2, /device:TPU:1, one launch (start us, length us, event | category | flops | bytes accessed | tf_op | source)
XLA Modules:
  0.0 73.7 jit_solution(3886185740204943543)
XLA Ops:
  0.0 72.2 %shard_map.46 = f32[64,256]{1,0:T(8,128)} custom-call(bf16[4,256,512]{2,1,0:T(8,128)(2,1)} %series_ref.1, s32[1,256]{1,0:T(1,128)} %bitcast.7, s32[13,256]{1,0:T(8,128)} %bitcast.6, f32[64,256]{1,0:T(8,128)} %bitcast.5), custom_call_target="tpu_custom_call" | custom-call | tf_op jit(solution)/shard_map/pallas_call | solution.py:487
  72.2 1.5 %copy.6 = f32[256,64]{0,1:T(8,128)} copy(f32[256,64]{0,1:T(8,128)} %bitcast.4) | data formatting | bytes 131072

commit v3 on v2

--- a/solution.py
+++ b/solution.py
@@ -78,8 +78,10 @@
     nhigh,
     nlow,
     scale_row,
-    scale_prev,
-    scale_next,
+    shares,
+    shares_prev,
+    shares_next,
+    shares_second,
     halo_out,
     from_prev,
     from_next,
@@ -87,8 +89,6 @@
     stage1,
     half,
     stage2,
-    whole,
-    other,
     in_sems,
     send,
     recv,
@@ -100,7 +100,6 @@
     s1_recv,
     s2_send,
     s2_recv,
-    s3_sems,
 ):
     groups, plane, planes, scale_factor = sizes
     count = plane * planes
@@ -113,16 +112,14 @@
     group = lax.axis_index("subj")
     spot = lax.rem(me, plane)
     level = me // plane
-    core = lax.rem(me, 2)
     following = {"vox": lax.rem(me + 1, count)}
     previous = {"vox": lax.rem(me + count - 1, count)}
-    partner = {"vox": me + 1 - 2 * core}
+    second = {"vox": lax.rem(me + count - 2, count)}
 
     plane_peers = [lax.rem(spot + d, plane) for d in range(1, plane)]
     level_peers = [lax.rem(level + d, planes) for d in range(1, planes)]
     group_peers = [lax.rem(group + d, groups) for d in range(1, groups)]
 
-    order = [0] + list(range(subjects - 1, 0, -1))
     loads = [
         pltpu.make_async_copy(series_ref.at[s], raw.at[s], in_sems.at[s])
         for s in range(subjects)
@@ -132,14 +129,11 @@
         pltpu.make_async_copy(mask_ref, live, in_sems.at[subjects + 1]),
         pltpu.make_async_copy(start_ref, begin, in_sems.at[subjects + 2]),
     ]
-    loads[0].start()
-    for load in small:
+    for load in loads + small:
         load.start()
-    for s in order[1:]:
-        loads[s].start()
 
     barrier = pltpu.get_barrier_semaphore()
-    targets = [following, previous]
+    targets = [following, previous, {"vox": lax.rem(me + 2, count)}, second]
     targets += [{"vox": level * plane + p} for p in plane_peers]
     targets += [{"vox": p * plane + spot} for p in level_peers]
     targets += [{"subj": p} for p in group_peers]
@@ -172,27 +166,19 @@
             zown[2 * s + 1, r : r + step, :] = result[:, width:]
 
     with jax.named_scope("zscore"):
-        loads[0].wait()
-        standardize(0)
-        with jax.named_scope("barrier"):
-            pl.semaphore_wait(barrier, len(targets))
-        first_on = single(0, zown.at[0:2], zahead.at[0:2], following)
-        first_on.start()
+        for s in range(subjects):
+            loads[s].wait()
+            standardize(s)
         for load in small:
             load.wait()
-        near_copy = single(3, near, near_next, previous)
-        near_copy.start()
-        turn = passed // 2
-        for s in order[1 : subjects - turn + 1]:
-            loads[s].wait()
-            standardize(s)
-        back_copy = single(2, zown.at[passed:halves], zback, previous)
-        back_copy.start()
-        for s in order[subjects - turn + 1 :]:
-            loads[s].wait()
-            standardize(s)
-        rest_on = single(1, zown.at[2:passed], zahead.at[2:passed], following)
-        rest_on.start()
+    with jax.named_scope("barrier"):
+        pl.semaphore_wait(barrier, len(targets))
+    back_copy = single(2, zown.at[passed:halves], zback, previous)
+    first_on = single(0, zown.at[0:2], zahead.at[0:2], following)
+    rest_on = single(1, zown.at[2:passed], zahead.at[2:passed], following)
+    near_copy = single(3, near, near_next, previous)
+    for copy in (near_copy, back_copy, first_on, rest_on):
+        copy.start()
 
     def products(left, right, first, last, left_first=0, right_first=0):
         total = None
@@ -298,20 +284,22 @@
     ones = jnp.ones((8, voxels), jnp.bfloat16)
     with jax.named_scope("dense"):
         dense(near, listed, ghigh, glow, 2 * voxels)
-        owed = matmul(ones, ghigh[voxels:, :], NT) + matmul(ones, glow[voxels:, :], NT)
+        owed = matmul(ones, ghigh[...], NT) + matmul(ones, glow[...], NT)
+        shares[:1, :] = (
+            1.0 + jnp.sum(listed[...], axis=0, keepdims=True) + owed[:1, voxels:]
+        )
+        shares[1:2, :] = owed[:1, :voxels]
+    share_copies = [
+        single(6, shares, shares_prev, following),
+        single(7, shares, shares_next, previous),
+        single(8, shares, shares_second, second),
+    ]
+    for copy in share_copies:
+        copy.start()
     with jax.named_scope("wait_list"):
         list_copy.wait_recv()
-    with jax.named_scope("degree"):
+    with jax.named_scope("dense_next"):
         dense(near_next, listed_next, nhigh, nlow, voxels)
-        owed = owed + (matmul(ones, nhigh[...], NT) + matmul(ones, nlow[...], NT))
-        degree = 1.0 + jnp.sum(listed[...], axis=0, keepdims=True) + owed[:1, :]
-        scale_row[...] = live[...].astype(jnp.float32) * lax.rsqrt(degree)
-    scale_copies = [
-        single(6, scale_row, scale_prev, following),
-        single(7, scale_row, scale_next, previous),
-    ]
-    for copy in scale_copies:
-        copy.start()
 
     def stacked(values):
         high, low = split(values)
@@ -334,19 +322,27 @@
         total = own + (mine[:vecs] + mine[vecs:] + rest)
         return 0.5 * (current + scale_row[...] * total)
 
-    own = own_part(vectors)
-    with jax.named_scope("wait_scale"):
-        for copy in scale_copies + list(halo(0)):
+    with jax.named_scope("wait_shares"):
+        for copy in share_copies + list(halo(0)):
             copy.wait_recv()
-    images = whole_part(
-        vectors, own, scale_prev[...] * from_prev[0], scale_next[...] * from_next[0]
-    )
-
-    lane = lax.broadcasted_iota(jnp.int32, (vecs // 2, 2 * vecs), 1)
+    with jax.named_scope("images0"):
+        scale_row[...] = live[...].astype(jnp.float32) * lax.rsqrt(
+            shares[:1, :] + shares_next[1:2, :]
+        )
+        scale_prev = lax.rsqrt(shares_prev[:1, :] + shares[1:2, :])
+        scale_next = lax.rsqrt(shares_next[:1, :] + shares_second[1:2, :])
+        images = whole_part(
+            vectors, own_part(vectors), scale_prev * from_prev[0], scale_next * from_next[0]
+        )
+
+    mid = vecs // 2
+    lane = lax.broadcasted_iota(jnp.int32, (mid, 2 * vecs), 1)
+    row = lax.broadcasted_iota(jnp.int32, (mid, 2 * vecs), 0)
+    column = lax.rem(lane, vecs)
     row_all = lax.broadcasted_iota(jnp.int32, (vecs, 2 * vecs), 0)
     lane_all = lax.broadcasted_iota(jnp.int32, (vecs, 2 * vecs), 1)
     identity = (lane_all - vecs == row_all).astype(jnp.float32)
-    quarter = vecs // 4
+    fold = mid // 2
 
     def send_halo(t, current):
         halo_out[t] = scale_row[...] * current
@@ -362,10 +358,9 @@
 
     def stage1_copy(t, d, arriving=False):
         peer = plane_peers[d]
-        source = gram.at[t, pl.ds(pl.multiple_of(lax.rem(peer, 2) * quarter, quarter), quarter)]
         target = {"vox": level * plane + peer}
         slot = peer if arriving else spot
-        return remote(source, stage1.at[t, slot], s1_send.at[t, d], s1_recv.at[t, slot], target)
+        return remote(gram.at[t], stage1.at[t, slot], s1_send.at[t, d], s1_recv.at[t, slot], target)
 
     def stage2_copy(t, d, arriving=False):
         peer = level_peers[d]
@@ -373,17 +368,18 @@
         slot = peer if arriving else level
         return remote(half.at[t], stage2.at[t, slot], s2_send.at[t, d], s2_recv.at[t, slot], target)
 
-    def stage3_copy(t):
-        return remote(whole.at[t], other.at[t], s3_sems.at[t, 0], s3_sems.at[t, 1], partner)
-
     def sum_start(t, current):
-        twice = jnp.concatenate([current, current], axis=0)
-        product = matmul(current, twice, NT, HIGHEST)
-        gram[t] = jnp.where(lane < vecs, product[: vecs // 2], product[vecs // 2 :])
+        upper, lower = current[:mid], current[mid:]
+        first = matmul(upper, jnp.concatenate([upper, lower] * 2, axis=0), NT, HIGHEST)
+        last = matmul(lower, jnp.concatenate([lower] * 4, axis=0), NT, HIGHEST)
+        square = jnp.where((column < mid) & (row < column), last, first)
+        gram[t, : fold, :] = jnp.where(lane[:fold] < vecs, square[:fold], square[fold:])
+        gram[t, fold : fold + 1, :] = jnp.sum(
+            jnp.where(row == column, last, 0.0), axis=0, keepdims=True
+        )
         for d in range(plane - 1):
             stage1_copy(t, d).start()
-        own_rows = pl.ds(pl.multiple_of(core * quarter, quarter), quarter)
-        stage1[t, spot] = gram[t, own_rows]
+        stage1[t, spot] = gram[t]
 
     def sum_planes(t):
         with jax.named_scope(f"s1_wait{t}"):
@@ -397,24 +393,23 @@
             stage2_copy(t, d).start()
         stage2[t, level] = total
 
-    def sum_levels(t):
+    def sum_end(t):
         with jax.named_scope(f"s2_wait{t}"):
             for d in range(planes - 1):
                 stage2_copy(t, d, True).wait_recv()
         total = stage2[t, 0]
         for p in range(1, planes):
             total = total + stage2[t, p]
-        whole[t] = total
-        stage3_copy(t).start()
-
-    def sum_end(t):
-        with jax.named_scope(f"s3_wait{t}"):
-            stage3_copy(t).wait_recv()
-        total, got = whole[t], other[t]
-        upper = jnp.where(core == 0, total, got)
-        lower = jnp.where(core == 0, got, total)
-        full = jnp.concatenate([upper, lower], axis=0)
-        return jnp.concatenate([full, pltpu.roll(full, vecs, 1)], axis=0)
+        folded, diagonal = total[:fold], total[fold : fold + 1]
+        square = jnp.concatenate([folded, pltpu.roll(folded, vecs, 1)], axis=0)
+        filled = jnp.concatenate(
+            [square, jnp.zeros((2 * vecs - mid, 2 * vecs), jnp.float32)], axis=0
+        )
+        turned = filled.T
+        top = jnp.where((lane < mid) & (row < lane), turned[:mid], square)
+        corner = jnp.where(row < lane, square, jnp.where(row == lane, diagonal, turned[:mid]))
+        bottom = jnp.where(lane < mid, turned[mid:vecs], pltpu.roll(corner, mid, 1))
+        return jnp.concatenate([top, bottom], axis=0)
 
     def inverse_factor(matrix):
         solved = factor_inverse(jnp.where(lane_all < vecs, matrix, identity))
@@ -430,22 +425,19 @@
     sum_planes(0)
     images = next_images(1, images)
     sum_start(1, images)
-    sum_levels(0)
+    matrix = sum_end(0)
     sum_planes(1)
-    matrix = sum_end(0)
     with jax.named_scope("chol0"):
         inverse = inverse_factor(matrix)
     images = matmul(inverse, images, NN, HIGHEST)
     send_halo(2, images)
     images = next_images(2, images)
     sum_start(2, images)
-    sum_levels(1)
+    matrix = sum_end(1)
     sum_planes(2)
-    matrix = sum_end(1)
     with jax.named_scope("chol1"):
         inverse = inverse_factor(normalized(inverse, matrix))
     images = matmul(inverse, images, NN, HIGHEST)
-    sum_levels(2)
     matrix = sum_end(2)
     with jax.named_scope("chol2"):
         inverse = inverse_factor(normalized(inverse, matrix))
@@ -453,7 +445,7 @@
 
     with jax.named_scope("tail"):
         singles = [first_on, rest_on, back_copy, near_copy, next_copy, list_copy]
-        for copy in singles + scale_copies + part_copies:
+        for copy in singles + share_copies + part_copies:
             copy.wait_send()
         for t in range(ITERS):
             for copy in halo(t):
@@ -462,7 +454,6 @@
                 stage1_copy(t, d).wait_send()
             for d in range(planes - 1):
                 stage2_copy(t, d).wait_send()
-            stage3_copy(t).wait_send()
 
 
 def solution(mesh):
@@ -479,15 +470,15 @@
         block = (vecs, voxels)
         table = (offsets, voxels)
         line = (1, voxels)
-        quarter = (vecs // 4, 2 * vecs)
+        packed = (vecs // 4 + 1, 2 * vecs)
         halves, width = 2 * subjects, frames // 2
-        passed = halves * 5 // 8
+        passed = halves * 3 // 4
         dma = pltpu.SemaphoreType.DMA
-        anywhere = pl.BlockSpec(memory_space=pl.ANY)
+        outside = pl.BlockSpec(memory_space=pltpu.HBM)
         result = pl.pallas_call(
             functools.partial(kernel, (groups, plane, planes, scale_factor)),
             out_shape=jax.ShapeDtypeStruct(block, f32),
-            in_specs=[anywhere] * 4,
+            in_specs=[outside] * 4,
             out_specs=pl.BlockSpec(memory_space=pltpu.VMEM),
             scratch_shapes=[
                 pltpu.VMEM((subjects, voxels, frames), bf16),
@@ -511,20 +502,20 @@
                 pltpu.VMEM((voxels, voxels), bf16),
                 pltpu.VMEM((voxels, voxels), bf16),
                 pltpu.VMEM(line, f32),
-                pltpu.VMEM(line, f32),
-                pltpu.VMEM(line, f32),
+                pltpu.VMEM((2, voxels), f32),
+                pltpu.VMEM((2, voxels), f32),
+                pltpu.VMEM((2, voxels), f32),
+                pltpu.VMEM((2, voxels), f32),
                 pltpu.VMEM((ITERS, *block), f32),
                 pltpu.VMEM((ITERS, *block), f32),
                 pltpu.VMEM((ITERS, *block), f32),
-                pltpu.VMEM((ITERS, vecs // 2, 2 * vecs), f32),
-                pltpu.VMEM((ITERS, plane, *quarter), f32),
-                pltpu.VMEM((ITERS, *quarter), f32),
-                pltpu.VMEM((ITERS, planes, *quarter), f32),
-                pltpu.VMEM((ITERS, *quarter), f32),
-                pltpu.VMEM((ITERS, *quarter), f32),
+                pltpu.VMEM((ITERS, *packed), f32),
+                pltpu.VMEM((ITERS, plane, *packed), f32),
+                pltpu.VMEM((ITERS, *packed), f32),
+                pltpu.VMEM((ITERS, planes, *packed), f32),
                 dma((subjects + 3,)),
-                dma((8,)),
-                dma((8,)),
+                dma((9,)),
+                dma((9,)),
                 dma((max(groups - 1, 1),)),
                 dma((groups,)),
                 dma((ITERS, 2)),
@@ -533,12 +524,18 @@
                 dma((ITERS, plane)),
                 dma((ITERS, planes - 1)),
                 dma((ITERS, planes)),
-                dma((ITERS, 2)),
             ],
             compiler_params=pltpu.CompilerParams(
-                collective_id=0, has_side_effects=True
+                collective_id=0, has_side_effects=True, vmem_limit_bytes=32 << 20
             ),
-        )(series, live_mask.reshape(1, voxels), neighbours.T, start_vectors.T)
+        )(
+            *(
+                pltpu.with_memory_space_constraint(operand, pltpu.HBM)
+                for operand in (
+                    series, live_mask.reshape(1, voxels), neighbours.T, start_vectors.T
+                )
+            )
+        )
         return result.T
 
     placed = (P("subj", "vox", None), P("vox"), P("vox", None), P("vox", None))

time: 73.9 us -> 70.3 us (0.951)
  Pallas kernels: 72.2 us -> 69.4 us
  local copies, waits for them, and re-layouts: 1.47 us -> 0.63 us
    pallas_call x1, Pallas kernels: 72.2 us -> 69.4 us  [on_device(): pl.pallas_call(functools.partial(kernel, (groups, plane, planes, scale_fa...]
    unnamed x1, local copies, waits for them, and re-layouts: 1.47 us -> 0.63 us
where the time goes in v3:
time: 70.3 us; the launch traced here: 70 us
  Pallas kernels  69.4 us (99%)
    pallas_call x1, Pallas kernels, on_device(): pl.pallas_call(functools.partial(kernel, (groups, plane, planes, scale_fa...  69.4 us

profile of v3, /device:TPU:1, one launch (start us, length us, event | category | flops | bytes accessed | tf_op | source)
XLA Modules:
  0.0 70.0 jit_solution(2366745926628315998)
XLA Ops:
  0.0 69.4 %shard_map.46 = f32[64,256]{1,0:T(8,128)S(1)} custom-call(bf16[4,256,512]{2,1,0:T(8,128)(2,1)} %series_ref.1, s32[1,256]{1,0:T(1,128)} %bitcast.7, s32[13,256]{1,0:T(8,128)} %bitcast.6, f32[64,256]{1,0:T(8,128)} %bitcast.5), custom_call_target="tpu_custom_call" | custom-call | tf_op jit(solution)/shard_map/pallas_call | solution.py:478
  69.4 0.6 copy.6

commit v4 on v3

--- a/solution.py
+++ b/solution.py
@@ -110,6 +110,7 @@
     passed = zahead.shape[0]
     me = lax.axis_index("vox")
     group = lax.axis_index("subj")
+    core = lax.rem(me, 2)
     spot = lax.rem(me, plane)
     level = me // plane
     following = {"vox": lax.rem(me + 1, count)}
@@ -175,10 +176,20 @@
         pl.semaphore_wait(barrier, len(targets))
     back_copy = single(2, zown.at[passed:halves], zback, previous)
     first_on = single(0, zown.at[0:2], zahead.at[0:2], following)
-    rest_on = single(1, zown.at[2:passed], zahead.at[2:passed], following)
+    rest_on = single(1, zown.at[2 : passed - 1], zahead.at[2 : passed - 1], following)
+    last_on = single(9, zown.at[passed - 1 : passed], zahead.at[passed - 1 : passed], following)
     near_copy = single(3, near, near_next, previous)
-    for copy in (near_copy, back_copy, first_on, rest_on):
-        copy.start()
+    ons = [first_on, rest_on, last_on]
+    backs = [near_copy, back_copy]
+
+    def start_for(parity, copies):
+        @pl.when(core == parity)
+        def _():
+            for copy in copies:
+                copy.start()
+
+    start_for(1, ons)
+    start_for(0, backs)
 
     def products(left, right, first, last, left_first=0, right_first=0):
         total = None
@@ -214,6 +225,8 @@
         down(sums, part)
         vectors = live[...].astype(jnp.float32) * begin[...]
         halo_out[0] = vectors
+    start_for(0, ons)
+    start_for(1, backs)
     with jax.named_scope("wait_first"):
         first_on.wait_recv()
     corr[:voxels, :] = products(zahead, zown, 0, 2)
@@ -227,8 +240,11 @@
     next_copy.start()
     with jax.named_scope("wait_rest"):
         rest_on.wait_recv()
+    corr[:voxels, :] += products(zahead, zown, 2, passed - 1)
+    with jax.named_scope("wait_last"):
+        last_on.wait_recv()
     with jax.named_scope("pick_cross"):
-        corr[:voxels, :] += products(zahead, zown, 2, passed)
+        corr[:voxels, :] += products(zahead, zown, passed - 1, passed)
         down(picked(corr, slots_of(near), 0, voxels, sums), part)
     with jax.named_scope("wait_part"):
         next_copy.wait_recv()
@@ -349,8 +365,7 @@
         for copy in halo(t):
             copy.start()
 
-    def next_images(t, current):
-        own = own_part(current)
+    def next_images(t, current, own):
         with jax.named_scope("wait_halo"):
             for copy in halo(t):
                 copy.wait_recv()
@@ -422,17 +437,19 @@
 
     sum_start(0, images)
     send_halo(1, images)
+    own = own_part(images)
     sum_planes(0)
-    images = next_images(1, images)
-    sum_start(1, images)
+    ahead = next_images(1, images, own)
+    sum_start(1, ahead)
+    send_halo(2, ahead)
+    own = own_part(ahead)
     matrix = sum_end(0)
     sum_planes(1)
     with jax.named_scope("chol0"):
         inverse = inverse_factor(matrix)
-    images = matmul(inverse, images, NN, HIGHEST)
-    send_halo(2, images)
-    images = next_images(2, images)
-    sum_start(2, images)
+    with jax.named_scope("images2"):
+        images = matmul(inverse, next_images(2, ahead, own), NN, HIGHEST)
+        sum_start(2, images)
     matrix = sum_end(1)
     sum_planes(2)
     with jax.named_scope("chol1"):
@@ -444,7 +461,7 @@
     out_ref[...] = matmul(inverse, images, NN, HIGHEST)
 
     with jax.named_scope("tail"):
-        singles = [first_on, rest_on, back_copy, near_copy, next_copy, list_copy]
+        singles = [first_on, rest_on, last_on, back_copy, near_copy, next_copy, list_copy]
         for copy in singles + share_copies + part_copies:
             copy.wait_send()
         for t in range(ITERS):
@@ -472,7 +489,7 @@
         line = (1, voxels)
         packed = (vecs // 4 + 1, 2 * vecs)
         halves, width = 2 * subjects, frames // 2
-        passed = halves * 3 // 4
+        passed = halves * 5 // 8
         dma = pltpu.SemaphoreType.DMA
         outside = pl.BlockSpec(memory_space=pltpu.HBM)
         result = pl.pallas_call(
@@ -514,8 +531,8 @@
                 pltpu.VMEM((ITERS, *packed), f32),
                 pltpu.VMEM((ITERS, planes, *packed), f32),
                 dma((subjects + 3,)),
-                dma((9,)),
-                dma((9,)),
+                dma((10,)),
+                dma((10,)),
                 dma((max(groups - 1, 1),)),
                 dma((groups,)),
                 dma((ITERS, 2)),

time: 70.3 us -> 66.8 us (0.950)
  the two profiles are of different devices: /device:TPU:1 before, /device:TPU:2 now
where the time goes in v4:
time: 66.8 us; the launch traced here: 66.6 us
  Pallas kernels  66 us (99%)
    pallas_call x1, Pallas kernels, on_device(): pl.pallas_call(functools.partial(kernel, (groups, plane, planes, scale_fa...  66 us

profile of v4, /device:TPU:2, one launch (start us, length us, event | category | flops | bytes accessed | tf_op | source)
XLA Modules:
  0.0 66.6 jit_solution(12185809568415038188)
XLA Ops:
  0.0 66.0 %shard_map.46 = f32[64,256]{1,0:T(8,128)S(1)} custom-call(bf16[4,256,512]{2,1,0:T(8,128)(2,1)} %series_ref.1, s32[1,256]{1,0:T(1,128)} %bitcast.7, s32[13,256]{1,0:T(8,128)} %bitcast.6, f32[64,256]{1,0:T(8,128)} %bitcast.5), custom_call_target="tpu_custom_call" | custom-call | tf_op jit(solution)/shard_map/pallas_call | solution.py:495
  66.0 0.6 copy.6

commit v5 on v4

--- a/solution.py
+++ b/solution.py
@@ -29,13 +29,20 @@
 def factor_inverse(rows):
     total, width = rows.shape
     sublane = lax.broadcasted_iota(jnp.int32, (8, width), 0)
-    done = []
-    for first in range(0, total, 8):
-        left = total - first
-        cols = [
+
+    def spread(first, left):
+        return [
             jnp.broadcast_to(rows[:, first + c : first + c + 1], (left, width))
             for c in range(8)
         ]
+
+    done = []
+    cols = spread(0, total)
+    for first in range(0, total, 8):
+        left = total - first
+        more = first + 8 < total
+        if more:
+            cols = cols + spread(first + 8, left)
         block = jnp.zeros((8, width), jnp.float32)
         for c in range(8):
             root = lax.rsqrt(cols[c][c : c + 1, :])
@@ -43,10 +50,11 @@
             pivot = rows[c : c + 1, :] * root
             block = jnp.where(sublane == c, pivot, block)
             rows = rows - lower * pivot
-            for other in range(c + 1, 8):
+            for other in range(c + 1, len(cols)):
                 cols[other] = cols[other] - lower * lower[other : other + 1, :]
         done.append(block)
         rows = rows[8:]
+        cols = [column[8:] for column in cols[8:]]
     return jnp.concatenate(done, axis=0)
 
 
@@ -73,6 +81,8 @@
     parts,
     listed,
     listed_next,
+    code,
+    code_next,
     ghigh,
     glow,
     nhigh,
@@ -121,6 +131,23 @@
     level_peers = [lax.rem(level + d, planes) for d in range(1, planes)]
     group_peers = [lax.rem(group + d, groups) for d in range(1, groups)]
 
+    barrier = pltpu.get_barrier_semaphore()
+    def far_first(peers):
+        return sorted(peers, key=lambda d: -min(d, len(peers) + 1 - d))
+
+    targets = []
+    for d in far_first(range(1, max(groups, planes))):
+        if d < groups:
+            targets.append({"subj": group_peers[d - 1]})
+        if d < planes:
+            targets.append({"vox": level_peers[d - 1] * plane + spot})
+    targets += [following, previous, {"vox": lax.rem(me + 2, count)}, second]
+    targets += [{"vox": level * plane + p} for p in plane_peers]
+    for target in targets:
+        pl.semaphore_signal(
+            barrier, inc=1, device_id=target, device_id_type=pl.DeviceIdType.MESH
+        )
+
     loads = [
         pltpu.make_async_copy(series_ref.at[s], raw.at[s], in_sems.at[s])
         for s in range(subjects)
@@ -132,16 +159,6 @@
     ]
     for load in loads + small:
         load.start()
-
-    barrier = pltpu.get_barrier_semaphore()
-    targets = [following, previous, {"vox": lax.rem(me + 2, count)}, second]
-    targets += [{"vox": level * plane + p} for p in plane_peers]
-    targets += [{"vox": p * plane + spot} for p in level_peers]
-    targets += [{"subj": p} for p in group_peers]
-    for target in targets:
-        pl.semaphore_signal(
-            barrier, inc=1, device_id=target, device_id_type=pl.DeviceIdType.MESH
-        )
 
     def remote(src, dst, send_sem, recv_sem, target):
         return pltpu.make_async_remote_copy(
@@ -218,6 +235,15 @@
         for k in range(offsets):
             target[k : k + 1, :] = jnp.sum(sums[k], axis=0, keepdims=True)
 
+    def number_edges(slots, codes, rows_total):
+        @pl.loop(0, rows_total // 8)
+        def _(r):
+            ids = tile + r * 8
+            number = jnp.full((8, voxels), 15, jnp.int32)
+            for k in range(offsets):
+                number = jnp.where(ids == slots[k], k, number)
+            codes[pl.ds(pl.multiple_of(r * 8, 8), 8), :] = number
+
     nothing = tuple(jnp.zeros((8, voxels), jnp.float32) for _ in range(offsets))
     with jax.named_scope("pick_own"):
         corr[voxels:, :] = products(zown, zown, 0, halves)
@@ -227,6 +253,7 @@
         halo_out[0] = vectors
     start_for(0, ons)
     start_for(1, backs)
+    number_edges(slots_of(near), code, 2 * voxels)
     with jax.named_scope("wait_first"):
         first_on.wait_recv()
     corr[:voxels, :] = products(zahead, zown, 0, 2)
@@ -238,6 +265,7 @@
         down(picked(corr_next, slots_of(near_next), 0, voxels, nothing), part_next)
     next_copy = single(4, part_next, part_in, following)
     next_copy.start()
+    number_edges(slots_of(near_next), code_next, voxels)
     with jax.named_scope("wait_rest"):
         rest_on.wait_recv()
     corr[:voxels, :] += products(zahead, zown, 2, passed - 1)
@@ -280,18 +308,33 @@
     list_copy = single(5, listed, listed_next, previous)
     list_copy.start()
 
-    def dense(near_table, weight_table, high_out, low_out, rows_total):
-        slots, weights = slots_of(near_table), slots_of(weight_table)
-
-        @pl.loop(0, rows_total // 16)
+    def dense(codes, weight_table, high_out, low_out, rows_total):
+        first = weight_table[:8, :]
+        second_rows = jnp.concatenate(
+            [weight_table[8:offsets, :], jnp.zeros((16 - offsets, voxels), jnp.float32)], axis=0
+        )
+
+        def gathered(source, index):
+            return jnp.concatenate(
+                [
+                    jnp.take_along_axis(
+                        source[:, c : c + 128], index[:, c : c + 128], axis=0,
+                        mode="promise_in_bounds",
+                    )
+                    for c in range(0, voxels, 128)
+                ],
+                axis=1,
+            )
+
+        @pl.loop(0, rows_total // 16, unroll=2)
         def _(r):
             tiles = []
             for h in range(2):
-                ids = tile + (r * 16 + h * 8)
-                entry = jnp.zeros((8, voxels), jnp.float32)
-                for k in range(offsets):
-                    entry = jnp.where(ids == slots[k], weights[k], entry)
-                tiles.append(entry)
+                number = codes[pl.ds(pl.multiple_of(r * 16 + h * 8, 8), 8), :]
+                inner = number & 7
+                tiles.append(
+                    jnp.where(number < 8, gathered(first, inner), gathered(second_rows, inner))
+                )
             high, low = split(jnp.concatenate(tiles, axis=0))
             rows = pl.ds(pl.multiple_of(r * 16, 16), 16)
             high_out[rows, :] = high
@@ -299,7 +342,7 @@
 
     ones = jnp.ones((8, voxels), jnp.bfloat16)
     with jax.named_scope("dense"):
-        dense(near, listed, ghigh, glow, 2 * voxels)
+        dense(code, listed, ghigh, glow, 2 * voxels)
         owed = matmul(ones, ghigh[...], NT) + matmul(ones, glow[...], NT)
         shares[:1, :] = (
             1.0 + jnp.sum(listed[...], axis=0, keepdims=True) + owed[:1, voxels:]
@@ -315,7 +358,7 @@
     with jax.named_scope("wait_list"):
         list_copy.wait_recv()
     with jax.named_scope("dense_next"):
-        dense(near_next, listed_next, nhigh, nlow, voxels)
+        dense(code_next, listed_next, nhigh, nlow, voxels)
 
     def stacked(values):
         high, low = split(values)
@@ -514,6 +557,8 @@
                 pltpu.VMEM((groups, *table), f32),
                 pltpu.VMEM(table, f32),
                 pltpu.VMEM(table, f32),
+                pltpu.VMEM((2 * voxels, voxels), i32),
+                pltpu.VMEM((voxels, voxels), i32),
                 pltpu.VMEM((2 * voxels, voxels), bf16),
                 pltpu.VMEM((2 * voxels, voxels), bf16),
                 pltpu.VMEM((voxels, voxels), bf16),

time: 66.8 us -> 65.4 us (0.979)
  the two profiles are of different devices: /device:TPU:2 before, /device:TPU:1 now
where the time goes in v5:
time: 65.4 us; the launch traced here: 64.2 us
  Pallas kernels  63.5 us (97%)
    pallas_call x1, Pallas kernels, on_device(): pl.pallas_call(functools.partial(kernel, (groups, plane, planes, scale_fa...  63.5 us

profile of v5, /device:TPU:1, one launch (start us, length us, event | category | flops | bytes accessed | tf_op | source)
XLA Modules:
  0.0 64.2 jit_solution(15748604612709160723)
XLA Ops:
  0.0 63.5 %shard_map.46 = f32[64,256]{1,0:T(8,128)S(1)} custom-call(bf16[4,256,512]{2,1,0:T(8,128)(2,1)} %series_ref.1, s32[1,256]{1,0:T(1,128)} %bitcast.7, s32[13,256]{1,0:T(8,128)} %bitcast.6, f32[64,256]{1,0:T(8,128)} %bitcast.5), custom_call_target="tpu_custom_call" | custom-call | tf_op jit(solution)/shard_map/pallas_call | solution.py:538
  63.5 0.6 copy.6

commit v6 on v5

--- a/solution.py
+++ b/solution.py
@@ -133,14 +133,14 @@
 
     barrier = pltpu.get_barrier_semaphore()
     def far_first(peers):
-        return sorted(peers, key=lambda d: -min(d, len(peers) + 1 - d))
+        return sorted(range(len(peers)), key=lambda d: -min(d + 1, len(peers) - d))
 
     targets = []
-    for d in far_first(range(1, max(groups, planes))):
-        if d < groups:
-            targets.append({"subj": group_peers[d - 1]})
-        if d < planes:
-            targets.append({"vox": level_peers[d - 1] * plane + spot})
+    for d in far_first(range(max(groups, planes) - 1)):
+        if d < groups - 1:
+            targets.append({"subj": group_peers[d]})
+        if d < planes - 1:
+            targets.append({"vox": level_peers[d] * plane + spot})
     targets += [following, previous, {"vox": lax.rem(me + 2, count)}, second]
     targets += [{"vox": level * plane + p} for p in plane_peers]
     for target in targets:
@@ -191,13 +191,17 @@
             load.wait()
     with jax.named_scope("barrier"):
         pl.semaphore_wait(barrier, len(targets))
-    back_copy = single(2, zown.at[passed:halves], zback, previous)
+    split_at = halves - passed - 1
+    back_copy = single(2, zown.at[passed : halves - 1], zback.at[0:split_at], previous)
+    back_last = single(
+        10, zown.at[halves - 1 : halves], zback.at[split_at : split_at + 1], previous
+    )
     first_on = single(0, zown.at[0:2], zahead.at[0:2], following)
     rest_on = single(1, zown.at[2 : passed - 1], zahead.at[2 : passed - 1], following)
     last_on = single(9, zown.at[passed - 1 : passed], zahead.at[passed - 1 : passed], following)
     near_copy = single(3, near, near_next, previous)
     ons = [first_on, rest_on, last_on]
-    backs = [near_copy, back_copy]
+    backs = [near_copy, back_copy, back_last]
 
     def start_for(parity, copies):
         @pl.when(core == parity)
@@ -260,8 +264,11 @@
     with jax.named_scope("wait_back"):
         near_copy.wait_recv()
         back_copy.wait_recv()
+    corr_next[...] = products(zown, zback, 0, split_at, left_first=passed)
+    with jax.named_scope("wait_back_last"):
+        back_last.wait_recv()
     with jax.named_scope("pick_next"):
-        corr_next[...] = products(zown, zback, 0, halves - passed, left_first=passed)
+        corr_next[...] += products(zown, zback, split_at, split_at + 1, left_first=passed)
         down(picked(corr_next, slots_of(near_next), 0, voxels, nothing), part_next)
     next_copy = single(4, part_next, part_in, following)
     next_copy.start()
@@ -279,9 +286,9 @@
     part[...] += part_in[...]
 
     part_copies = []
-    for d, peer in enumerate(group_peers):
+    for d in far_first(group_peers):
         copy = remote(
-            part, parts.at[group], part_send.at[d], part_recv.at[group], {"subj": peer}
+            part, parts.at[group], part_send.at[d], part_recv.at[group], {"subj": group_peers[d]}
         )
         copy.start()
         part_copies.append(copy)
@@ -435,7 +442,7 @@
         gram[t, fold : fold + 1, :] = jnp.sum(
             jnp.where(row == column, last, 0.0), axis=0, keepdims=True
         )
-        for d in range(plane - 1):
+        for d in far_first(plane_peers):
             stage1_copy(t, d).start()
         stage1[t, spot] = gram[t]
 
@@ -447,7 +454,7 @@
         for p in range(1, plane):
             total = total + stage1[t, p]
         half[t] = total
-        for d in range(planes - 1):
+        for d in far_first(level_peers):
             stage2_copy(t, d).start()
         stage2[t, level] = total
 
@@ -493,8 +500,8 @@
     with jax.named_scope("images2"):
         images = matmul(inverse, next_images(2, ahead, own), NN, HIGHEST)
         sum_start(2, images)
+    sum_planes(2)
     matrix = sum_end(1)
-    sum_planes(2)
     with jax.named_scope("chol1"):
         inverse = inverse_factor(normalized(inverse, matrix))
     images = matmul(inverse, images, NN, HIGHEST)
@@ -504,7 +511,7 @@
     out_ref[...] = matmul(inverse, images, NN, HIGHEST)
 
     with jax.named_scope("tail"):
-        singles = [first_on, rest_on, last_on, back_copy, near_copy, next_copy, list_copy]
+        singles = [first_on, rest_on, last_on, back_copy, back_last, near_copy, next_copy, list_copy]
         for copy in singles + share_copies + part_copies:
             copy.wait_send()
         for t in range(ITERS):
@@ -576,8 +583,8 @@
                 pltpu.VMEM((ITERS, *packed), f32),
                 pltpu.VMEM((ITERS, planes, *packed), f32),
                 dma((subjects + 3,)),
-                dma((10,)),
-                dma((10,)),
+                dma((11,)),
+                dma((11,)),
                 dma((max(groups - 1, 1),)),
                 dma((groups,)),
                 dma((ITERS, 2)),

time: 65.4 us -> 61.5 us (0.940); the launches traced: 64.2 us -> 61.4 us
  Pallas kernels: 63.5 us -> 60.7 us
    pallas_call x1, Pallas kernels: 63.5 us -> 60.7 us  [on_device(): pl.pallas_call(functools.partial(kernel, (groups, plane, planes, scale_fa...]
where the time goes in v6:
time: 61.5 us; the launch traced here: 61.4 us
  Pallas kernels  60.7 us (99%)
  local copies, waits for them, and re-layouts  0.63 us (1%)
    pallas_call x1, Pallas kernels, on_device(): pl.pallas_call(functools.partial(kernel, (groups, plane, planes, scale_fa...  60.7 us

profile of v6, /device:TPU:1, one launch (start us, length us, event | category | flops | bytes accessed | tf_op | source)
XLA Modules:
  0.0 61.4 jit_solution(15477294008249104477)
XLA Ops:
  0.0 60.7 %shard_map.46 = f32[64,256]{1,0:T(8,128)S(1)} custom-call(bf16[4,256,512]{2,1,0:T(8,128)(2,1)} %series_ref.1, s32[1,256]{1,0:T(1,128)} %bitcast.7, s32[13,256]{1,0:T(8,128)} %bitcast.6, f32[64,256]{1,0:T(8,128)} %bitcast.5), custom_call_target="tpu_custom_call" | custom-call | tf_op jit(solution)/shard_map/pallas_call | solution.py:545
  60.7 0.6 %copy.6 = f32[256,64]{0,1:T(8,128)} copy(f32[256,64]{0,1:T(8,128)S(1)} %bitcast.4) | data formatting | bytes 131072

commit v7 on v6

--- a/solution.py
+++ b/solution.py
@@ -224,20 +224,36 @@
     def slots_of(ref):
         return [jnp.broadcast_to(ref[k : k + 1, :], (8, voxels)) for k in range(offsets)]
 
-    def picked(source, slots, first, last, sums):
+    def gathered(source, index):
+        return jnp.concatenate(
+            [
+                jnp.take_along_axis(
+                    source[:, c : c + 128], index[:, c : c + 128], axis=0,
+                    mode="promise_in_bounds",
+                )
+                for c in range(0, voxels, 128)
+            ],
+            axis=1,
+        )
+
+    def picked(source, table, first, last, sums):
+        rest = jnp.full((16 - offsets, voxels), -1, jnp.int32)
+        slots = [table[:8, :], jnp.concatenate([table[8:offsets, :], rest], axis=0)]
+        inner = [slot & 7 for slot in slots]
+        outer = [lax.shift_right_arithmetic(slot, 3) for slot in slots]
+
         def body(r, sums):
-            ids = tile + r * 8
             values = source[pl.ds(pl.multiple_of(r * 8, 8), 8), :]
             return tuple(
-                total + jnp.where(ids == slots[k], values, 0.0)
-                for k, total in enumerate(sums)
+                jnp.where(outer[h] == r, gathered(values, inner[h]), total)
+                for h, total in enumerate(sums)
             )
 
-        return lax.fori_loop(first // 8, last // 8, body, sums, unroll=2)
+        return lax.fori_loop(first // 8, last // 8, body, sums, unroll=4)
 
     def down(sums, target):
-        for k in range(offsets):
-            target[k : k + 1, :] = jnp.sum(sums[k], axis=0, keepdims=True)
+        target[:8, :] = sums[0]
+        target[8:offsets, :] = sums[1][: offsets - 8]
 
     def number_edges(slots, codes, rows_total):
         @pl.loop(0, rows_total // 8)
@@ -248,11 +264,10 @@
                 number = jnp.where(ids == slots[k], k, number)
             codes[pl.ds(pl.multiple_of(r * 8, 8), 8), :] = number
 
-    nothing = tuple(jnp.zeros((8, voxels), jnp.float32) for _ in range(offsets))
+    nothing = tuple(jnp.zeros((8, voxels), jnp.float32) for _ in range(2))
     with jax.named_scope("pick_own"):
         corr[voxels:, :] = products(zown, zown, 0, halves)
-        sums = picked(corr, slots_of(near), voxels, 2 * voxels, nothing)
-        down(sums, part)
+        sums = picked(corr, near, voxels, 2 * voxels, nothing)
         vectors = live[...].astype(jnp.float32) * begin[...]
         halo_out[0] = vectors
     start_for(0, ons)
@@ -269,7 +284,7 @@
         back_last.wait_recv()
     with jax.named_scope("pick_next"):
         corr_next[...] += products(zown, zback, split_at, split_at + 1, left_first=passed)
-        down(picked(corr_next, slots_of(near_next), 0, voxels, nothing), part_next)
+        down(picked(corr_next, near_next, 0, voxels, nothing), part_next)
     next_copy = single(4, part_next, part_in, following)
     next_copy.start()
     number_edges(slots_of(near_next), code_next, voxels)
@@ -280,7 +295,7 @@
         last_on.wait_recv()
     with jax.named_scope("pick_cross"):
         corr[:voxels, :] += products(zahead, zown, passed - 1, passed)
-        down(picked(corr, slots_of(near), 0, voxels, sums), part)
+        down(picked(corr, near, 0, voxels, sums), part)
     with jax.named_scope("wait_part"):
         next_copy.wait_recv()
     part[...] += part_in[...]
@@ -320,18 +335,6 @@
         second_rows = jnp.concatenate(
             [weight_table[8:offsets, :], jnp.zeros((16 - offsets, voxels), jnp.float32)], axis=0
         )
-
-        def gathered(source, index):
-            return jnp.concatenate(
-                [
-                    jnp.take_along_axis(
-                        source[:, c : c + 128], index[:, c : c + 128], axis=0,
-                        mode="promise_in_bounds",
-                    )
-                    for c in range(0, voxels, 128)
-                ],
-                axis=1,
-            )
 
         @pl.loop(0, rows_total // 16, unroll=2)
         def _(r):
@@ -505,22 +508,22 @@
     with jax.named_scope("chol1"):
         inverse = inverse_factor(normalized(inverse, matrix))
     images = matmul(inverse, images, NN, HIGHEST)
+    singles = [first_on, rest_on, last_on, back_copy, back_last, near_copy, next_copy]
+    for copy in singles + [list_copy] + share_copies + part_copies:
+        copy.wait_send()
+    for t in range(ITERS):
+        for copy in halo(t):
+            copy.wait_send()
+        for d in range(plane - 1):
+            stage1_copy(t, d).wait_send()
+        for d in range(planes - 1 if t < ITERS - 1 else 0):
+            stage2_copy(t, d).wait_send()
     matrix = sum_end(2)
     with jax.named_scope("chol2"):
         inverse = inverse_factor(normalized(inverse, matrix))
     out_ref[...] = matmul(inverse, images, NN, HIGHEST)
-
-    with jax.named_scope("tail"):
-        singles = [first_on, rest_on, last_on, back_copy, back_last, near_copy, next_copy, list_copy]
-        for copy in singles + share_copies + part_copies:
-            copy.wait_send()
-        for t in range(ITERS):
-            for copy in halo(t):
-                copy.wait_send()
-            for d in range(plane - 1):
-                stage1_copy(t, d).wait_send()
-            for d in range(planes - 1):
-                stage2_copy(t, d).wait_send()
+    for d in range(planes - 1):
+        stage2_copy(ITERS - 1, d).wait_send()
 
 
 def solution(mesh):

time: 61.5 us -> 61 us (level)
  no operation moved by 1% of the time
where the time goes in v7:
time: 61 us; the launch traced here: 60.9 us
  Pallas kernels  60.2 us (99%)
  local copies, waits for them, and re-layouts  0.63 us (1%)
    pallas_call x1, Pallas kernels, on_device(): pl.pallas_call(functools.partial(kernel, (groups, plane, planes, scale_fa...  60.2 us

profile of v7, /device:TPU:1, one launch (start us, length us, event | category | flops | bytes accessed | tf_op | source)
XLA Modules:
  0.0 60.9 jit_solution(17722254458838207935)
XLA Ops:
  0.0 60.2 %shard_map.46 = f32[64,256]{1,0:T(8,128)S(1)} custom-call(bf16[4,256,512]{2,1,0:T(8,128)(2,1)} %series_ref.1, s32[1,256]{1,0:T(1,128)} %bitcast.7, s32[13,256]{1,0:T(8,128)} %bitcast.6, f32[64,256]{1,0:T(8,128)} %bitcast.5), custom_call_target="tpu_custom_call" | custom-call | tf_op jit(solution)/shard_map/pallas_call | solution.py:548
  60.2 0.6 %copy.6 = f32[256,64]{0,1:T(8,128)} copy(f32[256,64]{0,1:T(8,128)S(1)} %bitcast.4) | data formatting | bytes 131072

commit v8 on v7

--- a/solution.py
+++ b/solution.py
@@ -498,11 +498,10 @@
     own = own_part(ahead)
     matrix = sum_end(0)
     sum_planes(1)
-    with jax.named_scope("chol0"):
-        inverse = inverse_factor(matrix)
-    with jax.named_scope("images2"):
-        images = matmul(inverse, next_images(2, ahead, own), NN, HIGHEST)
-        sum_start(2, images)
+    beyond = next_images(2, ahead, own)
+    inverse = inverse_factor(matrix)
+    images = matmul(inverse, beyond, NN, HIGHEST)
+    sum_start(2, images)
     sum_planes(2)
     matrix = sum_end(1)
     with jax.named_scope("chol1"):

time: 61 us -> 61.6 us (level)
  no operation moved by 1% of the time
where the time goes in v8:
time: 61.6 us; the launch traced here: 61.4 us
  Pallas kernels  60.8 us (99%)
  local copies, waits for them, and re-layouts  0.63 us (1%)
    pallas_call x1, Pallas kernels, on_device(): pl.pallas_call(functools.partial(kernel, (groups, plane, planes, scale_fa...  60.8 us

profile of v8, /device:TPU:1, one launch (start us, length us, event | category | flops | bytes accessed | tf_op | source)
XLA Modules:
  0.0 61.4 jit_solution(16816666181273594082)
XLA Ops:
  0.0 60.8 %shard_map.46 = f32[64,256]{1,0:T(8,128)S(1)} custom-call(bf16[4,256,512]{2,1,0:T(8,128)(2,1)} %series_ref.1, s32[1,256]{1,0:T(1,128)} %bitcast.7, s32[13,256]{1,0:T(8,128)} %bitcast.6, f32[64,256]{1,0:T(8,128)} %bitcast.5), custom_call_target="tpu_custom_call" | custom-call | tf_op jit(solution)/shard_map/pallas_call | solution.py:547
  60.8 0.6 %copy.6 = f32[256,64]{0,1:T(8,128)} copy(f32[256,64]{0,1:T(8,128)S(1)} %bitcast.4) | data formatting | bytes 131072
